TPU v7x, 32 devices: a whole 2x2x4 slice. The times are simulated.
32 devices in a mesh: seq: 2 (over x), dp: 4 (over y, core), tp: 4 (over z).
Axes of the slice: x: 2, y: 2, z: 4, core: 2. Of those that a mesh axis runs over, the one named last changes fastest.
Arguments:
- patches: bfloat16 [16, 384, 1152], P(('dp', 'tp'), 'seq'), parts along dimension 0, may hold values from -6 to 6
- seg_ids: int32 [16, 384], P(('dp', 'tp'), 'seq'), parts along dimension 0, may hold values from 0 to 11, never falling along the last dimension, each value on 1 to 96 neighbouring positions
- pos_rows: int32 [16, 384], P(('dp', 'tp'), 'seq'), parts along dimension 0, may hold values from 0 to 63
- pos_cols: int32 [16, 384], P(('dp', 'tp'), 'seq'), parts along dimension 0, may hold values from 0 to 63
- row_table: bfloat16 [64, 1152], replicated, may hold values from -3 to 3
- col_table: bfloat16 [64, 1152], replicated, may hold values from -3 to 3
- ln1_gain: float32 [1152], replicated, may hold values from 0.5 to 1.5
- ln1_bias: float32 [1152], replicated, may hold values from -1.75 to 1.75
- w_qkv: bfloat16 [1152, 3456], P(None, 'seq'), may hold values from -0.41247896 to 0.41247896
- w_out: bfloat16 [1152, 1152], P('seq'), may hold values from -0.1875 to 0.1875
- out_bias: bfloat16 [1152], replicated, may hold values from -3 to 3
- ln2_gain: float32 [1152], replicated, may hold values from 0.5 to 1.5
- ln2_bias: float32 [1152], replicated, may hold values from -1.75 to 1.75
- w_fc1: bfloat16 [1152, 4304], P(None, 'tp'), may hold values from -0.1875 to 0.1875
- fc1_bias: bfloat16 [4304], P('tp'), may hold values from -3 to 3
- w_fc2: bfloat16 [4304, 1152], P('tp'), may hold values from -0.09375 to 0.09375
- fc2_bias: bfloat16 [1152], replicated, may hold values from -3 to 3
Outputs:
- encoded: bfloat16 [16, 384, 1152], P(('dp', 'tp'), 'seq'), parts along dimension 0
There are 4 independent parts, one for each index of `dp`. A program takes and returns all parts, laid end to end along the dimension named above; an argument that names none is the same for every part. Nothing has to cross between parts.
Inputs may be any that keep to these rules, and one draw needn't show every extreme that they name: `seg_ids`: image numbers never fall along a sequence; every image has 1 to 96 tokens.
All inputs are finite; a program needn't handle non-finite values.
Results may differ from a plain program's by a relative error of at most 0.0095.
Values may be sent and summed in bfloat16 or wider, within the bound.
No kernel may reach another device: no remote copies, remote signals or barrier semaphores. Data moves between devices by JAX's collectives and lax.ppermute only.
A program may use at most 64 MiB of HBM per device.

v0:
```python
import math

import jax
import jax.numpy as jnp
from jax import lax
from jax.sharding import PartitionSpec as P

HEADS = 16


def layer_norm(values, gain, shift):
    center = jnp.mean(values, -1, keepdims=True)
    spread = jnp.mean(jnp.square(values - center), -1, keepdims=True)
    return (values - center) * lax.rsqrt(spread + 1e-06) * gain + shift


def attend_head(item, segments):
    length = item.shape[0]
    head_dim = item.shape[1] // 3
    block = min(512, length)
    query = item[:, :head_dim].reshape(length // block, block, head_dim)
    seg_query = segments.reshape(length // block, block)
    keys = item[:, head_dim : 2 * head_dim]
    value = item[:, 2 * head_dim :]

    def one_block(pair):
        rows, seg_rows = pair
        scores = lax.dot_general(
            rows, keys, (((1,), (1,)), ((), ())), preferred_element_type=jnp.float32
        ) / math.sqrt(head_dim)
        same = seg_rows[:, None] == segments[None, :]
        scores = jnp.where(same, scores, -jnp.inf)
        top = jnp.max(scores, -1, keepdims=True)
        expo = jnp.exp(scores - top)
        probs = (expo / jnp.sum(expo, -1, keepdims=True)).astype(jnp.bfloat16)
        return jnp.dot(probs, value, preferred_element_type=jnp.float32).astype(jnp.bfloat16)

    return lax.map(one_block, (query, seg_query)).reshape(length, head_dim)


def per_device(
    patches,
    seg_ids,
    pos_rows,
    pos_cols,
    row_table,
    col_table,
    ln1_gain,
    ln1_bias,
    w_qkv,
    w_out,
    out_bias,
    ln2_gain,
    ln2_bias,
    w_fc1,
    fc1_bias,
    w_fc2,
    fc2_bias,
):
    width = patches.shape[2]
    head_dim = width // HEADS
    heads_here = w_qkv.shape[1] // (3 * head_dim)
    levels = jnp.arange(row_table.shape[0], dtype=jnp.int32)
    row_hot = (pos_rows[0][:, None] == levels[None, :]).astype(jnp.bfloat16)
    col_hot = (pos_cols[0][:, None] == levels[None, :]).astype(jnp.bfloat16)
    embedded = patches[0].astype(jnp.float32) + jnp.dot(
        row_hot, row_table, preferred_element_type=jnp.float32
    )
    embedded = embedded + jnp.dot(col_hot, col_table, preferred_element_type=jnp.float32)
    normed = layer_norm(embedded, ln1_gain, ln1_bias).astype(jnp.bfloat16)
    seg_all = lax.all_gather(seg_ids[0], "seq", axis=0, tiled=True)
    qkv = jnp.dot(
        lax.all_gather(normed, "seq", axis=0, tiled=True), w_qkv, preferred_element_type=jnp.float32
    ).astype(jnp.bfloat16)
    mixed = jax.vmap(attend_head, in_axes=(1, None), out_axes=1)(
        qkv.reshape(qkv.shape[0], heads_here, 3 * head_dim), seg_all
    )
    mixed = mixed.reshape(mixed.shape[0], heads_here * head_dim)
    rows = mixed
    projected = lax.psum_scatter(
        jnp.dot(rows, w_out, preferred_element_type=jnp.float32).astype(jnp.bfloat16),
        "seq",
        scatter_dimension=0,
        tiled=True,
    ).astype(jnp.float32)
    attended = embedded + projected + out_bias.astype(jnp.float32)
    normed2 = layer_norm(attended, ln2_gain, ln2_bias).astype(jnp.bfloat16)
    inner = jnp.dot(
        lax.all_gather(normed2, "tp", axis=0, tiled=True), w_fc1, preferred_element_type=jnp.float32
    ) + fc1_bias.astype(jnp.float32)
    hidden = jax.nn.gelu(inner, approximate=True).astype(jnp.bfloat16)
    rows = hidden
    reduced = lax.psum_scatter(
        jnp.dot(rows, w_fc2, preferred_element_type=jnp.float32).astype(jnp.bfloat16),
        "tp",
        scatter_dimension=0,
        tiled=True,
    ).astype(jnp.float32)
    encoded = (attended + reduced + fc2_bias.astype(jnp.float32)).astype(jnp.bfloat16)
    return encoded[None]


def solution(mesh):
    placed = (
        P(("dp", "tp"), "seq", None),
        P(("dp", "tp"), "seq"),
        P(("dp", "tp"), "seq"),
        P(("dp", "tp"), "seq"),
        P(),
        P(),
        P(),
        P(),
        P(None, "seq"),
        P("seq", None),
        P(),
        P(),
        P(),
        P(None, "tp"),
        P("tp"),
        P("tp", None),
        P(),
    )
    return jax.shard_map(
        per_device,
        mesh=mesh,
        in_specs=placed,
        out_specs=P(("dp", "tp"), "seq", None),
        check_vma=False,
    )
```

profile of v0, /device:TPU:0, one launch (start us, length us, event | category | flops | bytes accessed | tf_op | source)
XLA Modules:
  0.0 170.2 jit_solution(13854474931909000950)
XLA Ops:
  6.5 0.0 copy-start
  6.5 0.0 copy-start.2
  6.5 0.0 copy-start.1
  6.5 0.0 reduce-scatter.3.cloned.1.call-start
  6.6 0.0 copy-start.10
  6.6 0.0 copy-start.8
  6.6 1.6 convolution_add_fusion.2
  8.2 1.3 fusion.28
  9.5 0.2 multiply_reduce_fusion.1
  9.8 0.0 copy-done.2
  9.8 0.0 copy-done.1
  9.8 0.2 add_convert_fusion.2
  10.0 13.9 %all_gather.10 = bf16[384,1152]{1,0:T(8,128)(2,1)} all-gather(bf16[192,1152]{1,0:T(8,128)(2,1)S(1)} %add_convert_fusion.2), channel_id=1, replica_groups=mesh['seq'=2,'dp'=4,'tp'=4] {'seq'}, dimensions={0}, use_global_device_ids=true | all-gather | bytes 1327104 | tf_op jit(solution)/shard_map/all_gather | solution.py:73
  23.9 0.0 copy-done.10
  23.9 0.6 dynamic-slice.3
  25.2 0.0 copy-done.8
  25.2 0.2 dynamic-update-slice
  25.4 4.3 %all-reduce = s32[384]{0:T(512)S(1)} all-reduce(s32[384]{0:T(512)S(1)} %dynamic-update-slice), channel_id=2, replica_groups=mesh['seq'=2,'dp'=4,'tp'=4] {'seq'}, use_global_device_ids=true, to_apply=%add | all-reduce | flops 384 | bytes 3072 | tf_op jit(solution)/shard_map/all_gather | solution.py:71
  29.7 0.1 broadcast_compare_fusion
  29.8 5.9 %convolution_convert_fusion.1 = bf16[384,1728]{0,1:T(8,128)(2,1)} fusion(bf16[384,1152]{1,0:T(8,128)(2,1)} %all_gather.10, bf16[1152,1728]{0,1:T(8,128)(2,1)} %param.25), kind=kOutput, calls=%fused_computation.16 | convolution fusion | flops 1529487360 | bytes 6193152 | tf_op jit(solution)/shard_map/dot_general | solution.py:72
  35.7 4.9 %fusion.29 = (f32[8,384]{1,0:T(8,128)S(1)}, f32[8,384,384]{1,2,0:T(8,128)}) fusion(pred[384,384]{0,1:T(8,128)(4,1)S(1)} %broadcast_compare_fusion, bf16[384,8,216]{0,2,1:T(8,128)(2,1)} %bitcast.50), kind=kOutput, calls=%fused_computation.54 | convolution fusion | flops 174588288 | bytes 5763072 | tf_op jit(solution)/shard_map/vmap()/while/body/eval_jaxpr/sub | solution.py:34
  40.6 0.0 copy-start.9
  40.6 3.1 %fusion.14 = bf16[8,384,72]{1,2,0:T(8,128)(2,1)S(1)} fusion(f32[8,384,384]{1,2,0:T(8,128)} %get-tuple-element.20, f32[8,384]{1,0:T(8,128)S(1)} %get-tuple-element.19, bf16[384,8,216]{0,2,1:T(8,128)(2,1)} %bitcast.51), kind=kOutput, calls=%fused_computation.24 | convolution fusion | flops 172449792 | bytes 5615616 | tf_op jit(solution)/shard_map/vmap()/while/body/eval_jaxpr/dot_general | solution.py:36
  43.7 0.0 copy-start.5
  43.7 0.0 copy-done.9
  43.7 0.0 copy-start.3
  43.7 0.0 copy-start.4
  43.7 1.9 %convolution_convert_fusion.2 = bf16[384,1152]{1,0:T(8,128)(2,1)} fusion(bf16[384,576]{0,1:T(8,128)(2,1)S(1)} %bitcast.52, bf16[576,1152]{1,0:T(8,128)(2,1)S(1)} %copy-done.9), kind=kOutput, calls=%fused_computation.17 | convolution fusion | flops 510050304 | bytes 2654208 | tf_op jit(solution)/shard_map/dot_general | solution.py:81
  45.6 0.0 copy-start.6
  45.6 0.0 reduce-scatter.3.cloned.1.call-update
  45.6 0.0 all-gather.3.cloned.1.call-start
  45.7 0.0 copy-done.5
  45.7 20.2 %reduce-scatter.3.cloned.1.call-done = bf16[192,1152]{1,0:T(8,128)(2,1)} async-done(((bf16[384,1152]{1,0:T(8,128)(2,1)}), bf16[192,1152]{1,0:T(8,128)(2,1)}) %reduce-scatter.3.cloned.1.call-update) | async-done | bytes 442384 | tf_op jit(solution)/shard_map/reduce_scatter | solution.py:80
  65.9 1.2 fusion.27
  67.1 1.3 multiply_reduce_fusion
  68.4 0.0 copy-done.3
  68.4 0.0 copy-done.4
  68.4 2.0 %add_convert_fusion.1 = bf16[192,1152]{1,0:T(8,128)(2,1)} fusion(f32[1152]{0:T(1024)S(1)} %copy-done.3, f32[1152]{0:T(1024)S(1)} %copy-done.4, f32[192]{0:T(256)S(1)} %add_rsqrt_fusion, f32[192]{0:T(256)S(1)} %broadcast_multiply_fusion, f32[1152]{0:T(1024)S(1)} %convert_element_type.65, f32[192,1152]{1,0:T(8,128)S(1)} %get-tuple-element.18, ...), kind=kLoop, calls=%fused_computation.26 | loop fusion | flops 1769472 | bytes 1784832 | tf_op jit(solution)/shard_map/convert_element_type | solution.py:87
  70.5 0.0 all-gather.3.cloned.1.call-update
  70.5 0.2 reduce-scatter.5.cloned.1.call-start
  70.7 0.0 copy-done.6
  70.7 0.0 copy-start.7
  70.7 40.1 %all-gather.3.cloned.1.call-done = bf16[768,1152]{1,0:T(8,128)(2,1)} async-done(((bf16[192,1152]{1,0:T(8,128)(2,1)}), bf16[768,1152]{1,0:T(8,128)(2,1)}) %all-gather.3.cloned.1.call-update) | async-done | bytes 1769488 | tf_op jit(solution)/shard_map/all_gather | solution.py:89
  110.9 0.0 copy-done
  110.9 13.2 %convolution_convert_fusion = bf16[768,1152]{1,0:T(8,128)(2,1)} fusion(bf16[1076,1152]{1,0:T(8,128)(2,1)S(1)} %copy-done, bf16[768,1152]{1,0:T(8,128)(2,1)} %all-gather.3.cloned.1.call-done, bf16[1152,1076]{0,1:T(8,128)(2,1)} %param.30, f32[1076]{0:T(1024)S(1)} %convert_element_type.67), kind=kOutput, calls=%fused_computation.7 | convolution fusion | flops 3817052160 | bytes 8501456 | tf_op jit(solution)/shard_map/dot_general | solution.py:94
  124.1 0.0 reduce-scatter.5.cloned.1.call-update
  124.1 0.0 copy-done.7
  124.1 37.5 %reduce-scatter.5.cloned.1.call-done = bf16[192,1152]{1,0:T(8,128)(2,1)} async-done(((bf16[768,1152]{1,0:T(8,128)(2,1)}), bf16[192,1152]{1,0:T(8,128)(2,1)}) %reduce-scatter.5.cloned.1.call-update) | async-done | bytes 442384 | tf_op jit(solution)/shard_map/reduce_scatter | solution.py:93
  161.6 2.1 %fusion.17 = bf16[1,192,1152]{2,1,0:T(8,128)(2,1)} fusion(bf16[192,1152]{1,0:T(8,128)(2,1)} %reduce-scatter.5.cloned.1.call-done, f32[1152]{0:T(1024)S(1)} %convert_element_type.71, f32[1152]{0:T(1024)S(1)} %convert_element_type.65, f32[192,1152]{1,0:T(8,128)S(1)} %get-tuple-element.18, bf16[192,1152]{1,0:T(8,128)(2,1)} %reduce-scatter.3.cloned.1.call-done), kind=kLoop, calls=%fused_computation.32 | loop fusion | flops 1548288 | bytes 2221056 | tf_op jit(solution)/shard_map/broadcast_in_dim | solution.py:100
  (8 shorter events, 0.0 us)
Async XLA Ops:
  6.5 104.3 %copy-start = (bf16[1076,1152]{1,0:T(8,128)(2,1)S(1)}, bf16[1076,1152]{1,0:T(8,128)(2,1)}, u32[]{:S(2)}) copy-start(bf16[1076,1152]{1,0:T(8,128)(2,1)} %param.32) | copy-start | bytes 7437316
  6.5 3.2 %copy-start.2 = (f32[1152]{0:T(1024)S(1)}, f32[1152]{0:T(1024)}, u32[]{:S(2)}) copy-start(f32[1152]{0:T(1024)} %param.23) | copy-start | bytes 13828
  6.5 3.2 %copy-start.1 = (f32[1152]{0:T(1024)S(1)}, f32[1152]{0:T(1024)}, u32[]{:S(2)}) copy-start(f32[1152]{0:T(1024)} %param.24) | copy-start | bytes 13828
  6.5 59.4 %reduce-scatter.3.cloned.1.call-start = ((), (), s32[]{:S(2)}) async-start(), calls=%async_computation.2 | async-start | bytes 1327104 | tf_op jit(solution)/shard_map/reduce_scatter | solution.py:80
  6.6 17.4 %copy-start.10 = (u32[32]{0:T(128)S(1)}, u32[32]{0:T(128)}, u32[]{:S(2)}) copy-start(u32[32]{0:T(128)} %constant.45) | copy-start | bytes 388
  6.6 18.6 %copy-start.8 = (s32[1,192]{1,0:T(1,128)S(1)}, s32[1,192]{1,0:T(1,128)}, u32[]{:S(2)}) copy-start(s32[1,192]{1,0:T(1,128)} %param.18) | copy-start | bytes 2308
  40.6 3.1 %copy-start.9 = (bf16[576,1152]{1,0:T(8,128)(2,1)S(1)}, bf16[576,1152]{1,0:T(8,128)(2,1)}, u32[]{:S(2)}) copy-start(bf16[576,1152]{1,0:T(8,128)(2,1)} %param.26) | copy-start | bytes 3981316
  43.7 2.0 %copy-start.5 = (bf16[1152]{0:T(1024)(128)(2,1)S(1)}, bf16[1152]{0:T(1024)(128)(2,1)}, u32[]{:S(2)}) copy-start(bf16[1152]{0:T(1024)(128)(2,1)} %param.27) | copy-start | bytes 6916
  43.7 24.7 %copy-start.3 = (f32[1152]{0:T(1024)S(1)}, f32[1152]{0:T(1024)}, u32[]{:S(2)}) copy-start(f32[1152]{0:T(1024)} %param.29) | copy-start | bytes 13828
  43.7 24.7 %copy-start.4 = (f32[1152]{0:T(1024)S(1)}, f32[1152]{0:T(1024)}, u32[]{:S(2)}) copy-start(f32[1152]{0:T(1024)} %param.28) | copy-start | bytes 13828
  45.6 25.1 %copy-start.6 = (bf16[1076]{0:T(1024)(128)(2,1)S(1)}, bf16[1076]{0:T(1024)(128)(2,1)}, u32[]{:S(2)}) copy-start(bf16[1076]{0:T(1024)(128)(2,1)} %param.31) | copy-start | bytes 6460
  45.6 65.3 %all-gather.3.cloned.1.call-start = ((), (), s32[]{:S(2)}) async-start(), calls=%async_computation.3 | async-start | bytes 2211840 | tf_op jit(solution)/shard_map/all_gather | solution.py:89
  70.5 91.1 %reduce-scatter.5.cloned.1.call-start = ((), (), s32[]{:S(2)}) async-start(), calls=%async_computation.4 | async-start | bytes 2211840 | tf_op jit(solution)/shard_map/reduce_scatter | solution.py:93
  70.7 53.4 %copy-start.7 = (bf16[1152]{0:T(1024)(128)(2,1)S(1)}, bf16[1152]{0:T(1024)(128)(2,1)}, u32[]{:S(2)}) copy-start(bf16[1152]{0:T(1024)(128)(2,1)} %param.33) | copy-start | bytes 6916
Sparse Core Ops, SparseCore 0:
  45.7 20.1 reduce-scatter.2
  70.6 40.2 all-gather.2
  124.2 37.3 reduce-scatter.4
where the time goes:
time: 171 us; the launch traced here: 170 us
  waiting for transfers between devices  97.9 us (57%)
  matrix products  31.8 us (19%)
  blocking collectives  18.1 us (11%)
  between operations  14 us (8%)
  other arithmetic  7.26 us (4%)
    all_gather x1, waiting for transfers between devices, per_device(): lax.all_gather(normed2, 'tp', axis=0, tiled=True)  40.1 us
    reduce_scatter x1, waiting for transfers between devices, per_device(): lax.psum_scatter(jnp.dot(rows, w_fc2, preferred_element_type=jnp.float32)...  37.5 us
    reduce_scatter x1, waiting for transfers between devices, per_device(): lax.psum_scatter(jnp.dot(rows, w_out, preferred_element_type=jnp.float32)...  20.2 us
    all_gather x1, blocking collectives, per_device(): lax.all_gather(normed, 'seq', axis=0, tiled=True)  13.9 us
    dot_general x1, matrix products, per_device(): jnp.dot(rows, w_fc2, preferred_element_type=jnp.float32)  13.2 us
    dot_general x1, matrix products, per_device(): jnp.dot(lax.all_gather(normed, 'seq', axis=0, tiled=True), w_qkv, preferr...  5.87 us
    sub x1, matrix products, one_block(): expo = jnp.exp(scores - top)  4.94 us
    all_gather x1, blocking collectives, per_device(): seg_all = lax.all_gather(seg_ids[0], 'seq', axis=0, tiled=True)  4.25 us
  transfers between devices with their start and end apart: 3, of which 3 were waited for; matrix products, arithmetic and copies ran while one was open for 0% of the time, Pallas kernels for 0%

commit v1 on v0

--- a/solution.py
+++ b/solution.py
@@ -1,9 +1,13 @@
+import functools
 import math
 
 import jax
 import jax.numpy as jnp
 from jax import lax
+from jax.experimental import pallas as pl
+from jax.experimental.pallas import tpu as pltpu
 from jax.sharding import PartitionSpec as P
+
 
 HEADS = 16
 
@@ -38,7 +42,7 @@
     return lax.map(one_block, (query, seg_query)).reshape(length, head_dim)
 
 
-def per_device(
+def gathered_layer(
     patches,
     seg_ids,
     pos_rows,
@@ -100,6 +104,358 @@
     return encoded[None]
 
 
+def after(value, *earlier):
+    return lax.optimization_barrier((value,) + earlier)[0]
+
+
+def swap(values, axis, size, bit):
+    return lax.ppermute(values, axis, [(i, i ^ bit) for i in range(size)])
+
+
+def wide_dot(left, right):
+    return jnp.dot(left, right, preferred_element_type=jnp.float32)
+
+
+def dot_t(left, right):
+    return lax.dot_general(
+        left, right, (((1,), (1,)), ((), ())), preferred_element_type=jnp.float32
+    )
+
+
+def tn_dot(left, right):
+    return lax.dot_general(
+        left, right, (((0,), (0,)), ((), ())), preferred_element_type=jnp.float32
+    )
+
+
+def norm_rows(values, gain, shift):
+    center = jnp.mean(values, -1, keepdims=True)
+    moved = values - center
+    spread = jnp.mean(moved * moved, -1, keepdims=True)
+    return moved * lax.rsqrt(spread + 1e-06) * gain + shift
+
+
+def embed_kernel(patch, rows, cols, row_tab, col_tab, gain, shift, embedded, normed):
+    tokens = patch.shape[0]
+    grid = row_tab.shape[0]
+    level = lax.broadcasted_iota(jnp.int32, (grid, tokens), 0)
+    hot = jnp.concatenate([level == rows[...], level == cols[...]], 0)
+    hot = jnp.where(hot, 1.0, 0.0).astype(jnp.bfloat16)
+    table = jnp.concatenate([row_tab[...], col_tab[...]], 0)
+    values = patch[...].astype(jnp.float32) + tn_dot(hot, table)
+    embedded[...] = values
+    normed[...] = norm_rows(values, gain[...][None], shift[...][None]).astype(jnp.bfloat16)
+
+
+def qkv_kernel(normed, weight, out):
+    head_dim = out.shape[1]
+    product = dot_t(weight[...], normed[...])
+    for part in range(out.shape[0]):
+        out[part] = product[part * head_dim : (part + 1) * head_dim].astype(jnp.bfloat16)
+
+
+def column_of(row):
+    length = row.shape[1]
+    across = lax.broadcasted_iota(jnp.int32, (length, length), 0)
+    along = lax.broadcasted_iota(jnp.int32, (length, length), 1)
+    return jnp.sum(jnp.where(across == along, row, 0.0), -1, keepdims=True)
+
+
+def attend_kernel(near, far, seg_near, seg_far, weight, out, mixed):
+    head_dim = near.shape[1]
+    heads = near.shape[0] // 3
+    scale = math.log2(math.e) / math.sqrt(head_dim)
+    asked = seg_near[...].astype(jnp.float32)
+    same = [column_of(seg[...].astype(jnp.float32)) == asked for seg in (seg_near, seg_far)]
+    for head in range(heads):
+        query = near[3 * head]
+        scores = []
+        for side, keep in zip((near, far), same):
+            raw = tn_dot(side[3 * head + 1], query)
+            scores.append(jnp.where(keep, raw, -1e30))
+        top = jnp.maximum(
+            jnp.max(scores[0], 0, keepdims=True), jnp.max(scores[1], 0, keepdims=True)
+        )
+        total = 0.0
+        result = 0.0
+        for side, raw in zip((near, far), scores):
+            expo = jnp.exp2((raw - top) * scale)
+            total = total + jnp.sum(expo, 0, keepdims=True)
+            result = result + wide_dot(side[3 * head + 2], expo.astype(jnp.bfloat16))
+        mixed[head * head_dim : (head + 1) * head_dim, :] = result / total
+    out[...] = tn_dot(mixed[...].astype(jnp.bfloat16), weight[...]).astype(out.dtype)
+
+
+def join_kernel(embedded, kept, got, bias, gain, shift, attended, normed):
+    values = embedded[...] + (kept[...] + got[...].astype(jnp.float32))
+    values = values + bias[...].astype(jnp.float32)[None]
+    attended[...] = values
+    normed[...] = norm_rows(values, gain[...][None], shift[...][None]).astype(jnp.bfloat16)
+
+
+def gelu(values):
+    inner = values * (math.sqrt(2 / math.pi) + (math.sqrt(2 / math.pi) * 0.044715) * values * values)
+    half = 0.5 * values
+    return half + half * jnp.tanh(inner)
+
+
+def mlp_kernel(inputs, up, bias, down, total):
+    hidden = up.shape[0]
+    step = 512
+    for begin in range(0, hidden, step):
+        end = min(begin + step, hidden)
+        inner = dot_t(inputs[...], up[begin:end, :]) + bias[begin:end].astype(jnp.float32)[None]
+        piece = wide_dot(gelu(inner).astype(jnp.bfloat16), down[begin:end, :])
+        if begin == 0:
+            total[...] = piece
+        else:
+            total[...] += piece
+
+
+def far_mlp_kernel(count, place, inputs, bias, total, *refs):
+    ups, downs = refs[:count], refs[count : 2 * count]
+    rest = refs[2 * count :]
+    rows = ups[0].shape[0]
+    hidden = bias.shape[0]
+    line = bias[...].astype(jnp.float32)[None]
+    parts = [
+        line[:, begin : begin + rows]
+        for begin in [min(j * rows, hidden - rows) for j in range(count)]
+    ]
+    bit = 1
+    while bit < count:
+        turned = (place[0] // bit) % 2 == 1
+        parts = [jnp.where(turned, parts[j ^ bit], parts[j]) for j in range(count)]
+        bit *= 2
+    order = [step ^ core for core in (0, 1) for step in spread_order(count)]
+    up, down = rest[-2:]
+    for i in range(count):
+        up[i * rows : (i + 1) * rows, :] = ups[i][...]
+        down[i * rows : (i + 1) * rows, :] = downs[i][...]
+    result = total[...]
+    group = count // 2
+    for half in range(2):
+        begin, end = half * group * rows, (half + 1) * group * rows
+        shift = jnp.concatenate([parts[j] for j in order[half * group : (half + 1) * group]], 1)
+        inner = dot_t(inputs[...], up[begin:end, :]) + shift
+        result = result + wide_dot(gelu(inner).astype(jnp.bfloat16), down[begin:end, :])
+    if len(rest) > 3:
+        attended, last_bias, out = rest[:3]
+        out[...] = result + attended[...] + last_bias[...].astype(jnp.float32)[None]
+    else:
+        rest[0][...] = result.astype(jnp.bfloat16)
+
+
+def spread_order(holders):
+    return [0, holders // 2, 2, holders // 2 + 2]
+
+
+def run(kernel, room, out_shape, scratch=(), fetched=(), flops=0, scalars=()):
+    def call(*args):
+        args = list(args)
+        specs = []
+        buffers = []
+        for i, arg in enumerate(args):
+            if i in scalars:
+                specs.append(pl.BlockSpec(memory_space=pltpu.SMEM))
+            elif i in fetched:
+                args[i] = pltpu.with_memory_space_constraint(arg, pltpu.HBM)
+                specs.append(pl.BlockSpec(memory_space=pltpu.HBM))
+                buffers.append(pltpu.VMEM(arg.shape, arg.dtype))
+            else:
+                specs.append(pl.BlockSpec(memory_space=pltpu.VMEM))
+
+        def body(*refs):
+            refs = list(refs)
+            if fetched:
+                extra = refs[len(refs) - len(buffers) - 1 :]
+                refs = refs[: len(refs) - len(buffers) - 1]
+                copies = []
+                for slot, i in enumerate(fetched):
+                    copies.append(
+                        pltpu.make_async_copy(refs[i], extra[slot], extra[-1].at[slot])
+                    )
+                    refs[i] = extra[slot]
+                for copy in copies:
+                    copy.start()
+                for copy in copies:
+                    copy.wait()
+            kernel(*refs)
+
+        more = buffers + [pltpu.SemaphoreType.DMA((len(buffers),))] if fetched else []
+        return pl.pallas_call(
+            body,
+            in_specs=specs,
+            out_shape=out_shape,
+            scratch_shapes=list(scratch) + more,
+            compiler_params=pltpu.CompilerParams(vmem_limit_bytes=room << 20),
+            cost_estimate=pl.CostEstimate(flops=flops, bytes_accessed=0, transcendentals=0),
+        )(*args)
+
+    return call
+
+
+def swapped_layer(sizes):
+    seq, dp, tp = sizes
+
+    def per_device(
+        patches,
+        seg_ids,
+        pos_rows,
+        pos_cols,
+        row_table,
+        col_table,
+        ln1_gain,
+        ln1_bias,
+        w_qkv,
+        w_out,
+        out_bias,
+        ln2_gain,
+        ln2_bias,
+        w_fc1,
+        fc1_bias,
+        w_fc2,
+        fc2_bias,
+    ):
+        return steps(
+            patches,
+            seg_ids,
+            pos_rows,
+            pos_cols,
+            row_table,
+            col_table,
+            ln1_gain,
+            ln1_bias,
+            w_qkv,
+            w_out,
+            out_bias,
+            ln2_gain,
+            ln2_bias,
+            w_fc1,
+            fc1_bias,
+            w_fc2,
+            fc2_bias,
+        )
+
+    def steps(
+        patches,
+        seg_ids,
+        pos_rows,
+        pos_cols,
+        row_table,
+        col_table,
+        ln1_gain,
+        ln1_bias,
+        w_qkv,
+        w_out,
+        out_bias,
+        ln2_gain,
+        ln2_bias,
+        w_fc1,
+        fc1_bias,
+        w_fc2,
+        fc2_bias,
+    ):
+        tokens, width = patches.shape[1:]
+        head_dim = width // HEADS
+        heads_here = w_qkv.shape[1] // (3 * head_dim)
+        hidden = w_fc2.shape[0]
+        f32, bf16 = jnp.float32, jnp.bfloat16
+        block = (tokens, width)
+        sent_block = jax.ShapeDtypeStruct(block, bf16)
+        place = lax.axis_index("seq") * dp + lax.axis_index("dp")
+        holders = seq * dp
+        fc1_rows = w_fc1.T
+        qkv_rows = w_qkv.T
+        each = 2 * tokens * width
+
+        embedded, normed = run(
+            embed_kernel,
+            8,
+            (pltpu.VMEM(block, f32), sent_block),
+            fetched=tuple(range(7)),
+            flops=each * 256,
+        )(patches[0], pos_rows, pos_cols, row_table, col_table, ln1_gain, ln1_bias)
+        normed_other = swap(normed, "seq", seq, 1)
+        seg_other = swap(seg_ids, "seq", seq, 1)
+
+        rows = -(-hidden // (8 * holders)) * 8
+        overlap = rows * holders - hidden
+        begin = jnp.minimum(place * rows, hidden - rows)
+        share1 = lax.dynamic_slice(after(fc1_rows, normed), (begin, 0), (rows, width))
+        far1 = swap(share1, "tp", tp, 2)
+        share2 = lax.dynamic_slice(after(w_fc2, share1), (begin, 0), (rows, width))
+        repeated = (place == holders - 1) & (jnp.arange(rows) < overlap)
+        share2 = jnp.where(repeated[:, None], jnp.zeros_like(share2), share2)
+        far2 = swap(share2, "tp", tp, 2)
+        far_bias = swap(fc1_bias, "tp", tp, 2)
+
+        def project(values):
+            return run(
+                qkv_kernel,
+                8,
+                pltpu.VMEM((3 * heads_here, head_dim, tokens), bf16),
+                flops=each * qkv_rows.shape[0],
+            )(values, qkv_rows)
+
+        qkv_own = project(after(normed, share1))
+        qkv_other = project(normed_other)
+
+        def spread(share):
+            along_x = swap(share, "seq", seq, 1)
+            along_y = swap(share, "dp", dp, 2)
+            both = swap(share, ("seq", "dp"), seq * dp, dp + 2)
+            return [share, along_x, along_y, both]
+
+        def cross(shares):
+            return shares + [swap(share, "dp", dp, 1) for share in shares]
+
+        def attend(near, far, seg_near, seg_far, shape):
+            scratch = [pltpu.VMEM((heads_here * head_dim, tokens), f32)]
+            return run(attend_kernel, 8, shape, scratch, flops=each * 2304)(
+                near, far, seg_near, seg_far, w_out
+            )
+
+        sent = attend(qkv_other, qkv_own, seg_other, seg_ids, sent_block)
+        got = swap(sent, "seq", seq, 1)
+        near1 = spread(after(far1, sent))
+        kept = attend(
+            after(qkv_own, sent, far1, far_bias), qkv_other, seg_ids, seg_other, pltpu.VMEM(block, f32)
+        )
+        attended, normed2 = run(
+            join_kernel, 8, (pltpu.VMEM(block, f32), sent_block), fetched=(3, 4, 5), flops=each * 64
+        )(embedded, kept, got, out_bias, ln2_gain, ln2_bias)
+        partner = swap(normed2, "tp", tp, 1)
+        ups = cross([after(share, normed2) for share in near1])
+        near2 = spread(after(far2, normed2))
+
+        def mlp(values):
+            return run(
+                mlp_kernel, 8, pltpu.VMEM(block, f32), flops=2 * each * hidden
+            )(values, fc1_rows, fc1_bias, w_fc2)
+
+        mine = mlp(normed2)
+        theirs = mlp(partner)
+        downs = cross([after(share, partner) for share in near2])
+
+        def far_mlp(values, total, shape, *tail):
+            return run(
+                functools.partial(far_mlp_kernel, holders),
+                14,
+                shape,
+                [pltpu.VMEM((holders * rows, width), bf16)] * 2,
+                flops=2 * each * hidden,
+                scalars=(0,),
+            )(place[None], values, far_bias, total, *ups, *downs, *tail)
+
+        back = far_mlp(partner, theirs, sent_block)
+        returned = swap(back, "tp", tp, 1)
+        ours = far_mlp(after(normed2, back), mine, pltpu.VMEM(block, f32), attended, fc2_bias)
+        return (ours + returned.astype(f32)).astype(bf16)[None]
+
+    return per_device
+
+
 def solution(mesh):
     placed = (
         P(("dp", "tp"), "seq", None),
@@ -120,8 +476,11 @@
         P("tp", None),
         P(),
     )
+    sizes = mesh.shape["seq"], mesh.shape["dp"], mesh.shape["tp"]
+    swapped = sizes == (2, 4, 4)
+    layer = swapped_layer(sizes) if swapped else gathered_layer
     return jax.shard_map(
-        per_device,
+        layer,
         mesh=mesh,
         in_specs=placed,
         out_specs=P(("dp", "tp"), "seq", None),

time: 171 us -> 92.3 us (0.54)
  waiting for transfers between devices: 97.9 us -> 45.3 us
  matrix products: 31.8 us -> 0 us
  Pallas kernels: 0 us -> 21.5 us
  starting transfers between devices: 0.27 us -> 20.8 us
  blocking collectives: 18.1 us -> 0 us
  between operations: 14 us -> 0.23 us
  other arithmetic: 7.26 us -> 0.99 us
  local copies, waits for them, and re-layouts: 0.89 us -> 3.22 us
    reduce_scatter x2 -> x0, waiting for transfers between devices: 57.7 us -> none  [the longest x1 37.5 us: per_device(): lax.psum_scatter(jnp.dot(rows, w_fc2, preferred_element_type=jnp.float32)...]
    ppermute x0 -> x22, waiting for transfers between devices: none -> 45.3 us  [swap(): return lax.ppermute(values, axis, [(i, i ^ bit) for i in range(size)])]
    all_gather x1 -> x0, waiting for transfers between devices: 40.1 us -> none  [per_device(): lax.all_gather(normed2, 'tp', axis=0, tiled=True)]
    dot_general x6 -> x0, matrix products: 26.9 us -> none  [the longest x1 13.2 us: per_device(): jnp.dot(rows, w_fc2, preferred_element_type=jnp.float32)]
    pallas_call x0 -> x10, Pallas kernels: none -> 21.5 us  [call(): pl.pallas_call(body, in_specs=specs, out_shape=out_shape, scratch_shapes=...]
    ppermute x0 -> x22, starting transfers between devices: none -> 20.8 us  [swap(): return lax.ppermute(values, axis, [(i, i ^ bit) for i in range(size)])]
    all_gather x2 -> x0, blocking collectives: 18.1 us -> none  [the longest x1 13.9 us: per_device(): lax.all_gather(normed, 'seq', axis=0, tiled=True)]
    sub x1 -> x0, matrix products: 4.94 us -> none  [one_block(): expo = jnp.exp(scores - top)]
  transfers between devices with their start and end apart: 3 -> 22, of which waited for: 3 -> 9; matrix products, arithmetic and copies ran while one was open for 0% -> 1% of each run, Pallas kernels for 0% -> 19%
where the time goes in v1:
time: 92.3 us; the launch traced here: 92 us
  waiting for transfers between devices  45.3 us (49%)
  Pallas kernels  21.5 us (23%)
  starting transfers between devices  20.8 us (23%)
  local copies, waits for them, and re-layouts  3.22 us (3%)
  other arithmetic  0.99 us (1%)
    ppermute x22, waiting for transfers between devices, swap(): return lax.ppermute(values, axis, [(i, i ^ bit) for i in range(size)])  45.3 us
    pallas_call x10, Pallas kernels, call(): pl.pallas_call(body, in_specs=specs, out_shape=out_shape, scratch_shapes=...  21.5 us
    ppermute x22, starting transfers between devices, swap(): return lax.ppermute(values, axis, [(i, i ^ bit) for i in range(size)])  20.8 us
    unnamed x16, local copies, waits for them, and re-layouts  2.17 us
  transfers between devices with their start and end apart: 22, of which 9 were waited for; matrix products, arithmetic and copies ran while one was open for 1% of the time, Pallas kernels for 19%

profile of v1, /device:TPU:0, one launch (start us, length us, event | category | flops | bytes accessed | tf_op | source)
XLA Modules:
  0.0 92.0 jit_solution(6330498176583090614)
XLA Ops:
  0.0 1.8 %shard_map.163 = (f32[192,1152]{1,0:T(8,128)S(1)}, bf16[192,1152]{1,0:T(8,128)(2,1)S(1)}) custom-call(bf16[192,1152]{1,0:T(8,128)(2,1)} %bitcast.11, s32[1,192]{1,0:T(1,128)} %refs_1_.1, s32[1,192]{1,0:T(1,128)} %refs_2_.4, bf16[64,1152]{1,0:T(8,128)(2,1)} %refs_3_.5, bf16[64,1152]{1,0:T(8,128)(2,1)} %refs_4_.4, f32[1152]{0:T(1024)} %refs_5_.2, f32[1152]{0:T(1024)} %refs_6_.1), custom_call_target="tpu_custom_call" | custom-call | flops 113246208 | tf_op jit(solution)/shard_map/pallas_call | solution.py:286
  1.8 3.0 %collective-permute-start = (bf16[192,1152]{1,0:T(8,128)(2,1)S(1)}, bf16[192,1152]{1,0:T(8,128)(2,1)S(1)}, u32[]{:S(2)}, u32[]{:S(2)}) collective-permute-start(bf16[192,1152]{1,0:T(8,128)(2,1)S(1)} %get-tuple-element.27.refs_0_), channel_id=1, source_target_pairs={{0,16},{16,0},{1,17},{17,1},{2,18},{18,2},{3,19},{19,3},{4,20},{20... | collective-permute-start | bytes 1327112 | tf_op jit(solution)/shard_map/ppermute | solution.py:112
  4.9 0.1 collective-permute-start.1
  4.9 1.1 %constant_dynamic-slice_fusion = bf16[136,1152]{1,0:T(8,128)(2,1)S(1)} fusion(bf16[1076,1152]{1,0:T(8,128)(2,1)} %bitcast.8, s32[]{:T(128)S(6)} %select_n.8), kind=kLoop, calls=%fused_computation.4 | loop fusion | bytes 626692 | tf_op jit(solution)/shard_map/dynamic_slice | solution.py:385
  6.0 3.1 %collective-permute-start.2 = (bf16[136,1152]{1,0:T(8,128)(2,1)S(1)}, bf16[136,1152]{1,0:T(8,128)(2,1)S(1)}, u32[]{:S(2)}, u32[]{:S(2)}) collective-permute-start(bf16[136,1152]{1,0:T(8,128)(2,1)S(1)} %constant_dynamic-slice_fusion), channel_id=1, source_target_pairs={{0,2},{1,3},{2,0},{3,1},{4,6},{5,7},{6,4},{7,5},{8,10},{9,11},{10,... | collective-permute-start | bytes 940040 | tf_op jit(solution)/shard_map/ppermute | solution.py:112
  9.1 2.1 %copy-done = bf16[1152,1728]{0,1:T(8,128)(2,1)S(1)} copy-done((bf16[1152,1728]{0,1:T(8,128)(2,1)S(1)}, bf16[1152,1728]{0,1:T(8,128)(2,1)}, u32[]{:S(2)}) %copy-start) | copy-done | bytes 3981336
  11.2 1.3 %shard_map.164.refs_1_.refs_0_ = bf16[24,72,192]{2,1,0:T(8,128)(2,1)S(1)} custom-call(bf16[192,1152]{1,0:T(8,128)(2,1)S(1)} %get-tuple-element.27.refs_0_, bf16[1728,1152]{1,0:T(8,128)(2,1)S(1)} %bitcast.6), custom_call_target="tpu_custom_call" | custom-call | flops 764411904 | tf_op jit(solution)/shard_map/pallas_call | solution.py:286
  12.6 0.0 copy-start.4
  12.6 0.0 copy-start.7
  12.6 2.4 %collective-permute-done.refs_0_ = bf16[192,1152]{1,0:T(8,128)(2,1)S(1)} collective-permute-done((bf16[192,1152]{1,0:T(8,128)(2,1)S(1)}, bf16[192,1152]{1,0:T(8,128)(2,1)S(1)}, u32[]{:S(2)}, u32[]{:S(2)}) %collective-permute-start) | collective-permute-done | bytes 442400 | tf_op jit(solution)/shard_map/ppermute | solution.py:112
  15.1 1.3 %shard_map.165.refs_0_.refs_1_ = bf16[24,72,192]{2,1,0:T(8,128)(2,1)S(1)} custom-call(bf16[192,1152]{1,0:T(8,128)(2,1)S(1)} %collective-permute-done.refs_0_, bf16[1728,1152]{1,0:T(8,128)(2,1)S(1)} %bitcast.7), custom_call_target="tpu_custom_call" | custom-call | flops 764411904 | tf_op jit(solution)/shard_map/pallas_call | solution.py:286
  16.4 0.0 copy-start.3
  16.4 0.0 copy-start.5
  16.4 0.0 collective-permute-done.1.refs_2_.refs_3_
  16.5 3.2 %shard_map.166 = bf16[192,1152]{1,0:T(8,128)(2,1)S(1)} custom-call(bf16[24,72,192]{2,1,0:T(8,128)(2,1)S(1)} %shard_map.165.refs_0_.refs_1_, bf16[24,72,192]{2,1,0:T(8,128)(2,1)S(1)} %shard_map.164.refs_1_.refs_0_, s32[1,192]{1,0:T(1,128)S(1)} %collective-permute-done.1.refs_2_.refs_3_, s32[1,192]{1,0:T(1,128)S(1)} %copy-done.7, bf16[576,1152]{1,0:T(8,128)(2,1)S(1)} %copy-done.4), custom_call_target="tpu_custom_call" | custom-call | flops 1019215872 | tf_op jit(solution)/shard_map/pallas_call | solution.py:286
  19.6 1.8 %collective-permute-start.4 = (bf16[192,1152]{1,0:T(8,128)(2,1)S(1)}, bf16[192,1152]{1,0:T(8,128)(2,1)S(1)}, u32[]{:S(2)}, u32[]{:S(2)}) collective-permute-start(bf16[192,1152]{1,0:T(8,128)(2,1)S(1)} %shard_map.166), channel_id=1, source_target_pairs={{0,16},{16,0},{1,17},{17,1},{2,18},{18,2},{3,19},{19,3},{4,20},{20... | collective-permute-start | bytes 1327112 | tf_op jit(solution)/shard_map/ppermute | solution.py:112
  21.4 0.1 dynamic-slice_select_fusion
  21.5 0.0 copy-start.2
  21.6 2.6 %collective-permute-start.13 = (bf16[136,1152]{1,0:T(8,128)(2,1)S(1)}, bf16[136,1152]{1,0:T(8,128)(2,1)S(1)}, u32[]{:S(2)}, u32[]{:S(2)}) collective-permute-start(bf16[136,1152]{1,0:T(8,128)(2,1)S(1)} %dynamic-slice_select_fusion), channel_id=1, source_target_pairs={{0,2},{1,3},{2,0},{3,1},{4,6},{5,7},{6,4},{7,5},{8,10},{9,11},{10,... | collective-permute-start | bytes 940040 | tf_op jit(solution)/shard_map/ppermute | solution.py:112
  24.2 0.3 collective-permute-start.3
  24.6 12.9 %collective-permute-done.3.refs_2_ = bf16[1076]{0:T(1024)(128)(2,1)S(1)} collective-permute-done((bf16[1076]{0:T(1024)(128)(2,1)S(1)}, bf16[1076]{0:T(1024)(128)(2,1)S(1)}, u32[]{:S(2)}, u32[]{:S(2)}) %collective-permute-start.3) | collective-permute-done | bytes 2184 | tf_op jit(solution)/shard_map/ppermute | solution.py:112
  37.4 0.0 collective-permute-done.2.refs_4_
  37.4 3.2 %shard_map.167.refs_1_ = f32[192,1152]{1,0:T(8,128)S(1)} custom-call(bf16[24,72,192]{2,1,0:T(8,128)(2,1)S(1)} %shard_map.164.refs_1_.refs_0_, bf16[24,72,192]{2,1,0:T(8,128)(2,1)S(1)} %shard_map.165.refs_0_.refs_1_, s32[1,192]{1,0:T(1,128)S(1)} %copy-done.7, s32[1,192]{1,0:T(1,128)S(1)} %collective-permute-done.1.refs_2_.refs_3_, bf16[576,1152]{1,0:T(8,128)(2,1)S(1)} %copy-done.4), custom_call_target="tpu_custom_call" | custom-call | flops 1019215872 | tf_op jit(solution)/shard_map/pallas_call | solution.py:286
  40.6 0.0 collective-permute-done.4.refs_2_
  40.6 1.2 %shard_map.168 = (f32[192,1152]{1,0:T(8,128)S(1)}, bf16[192,1152]{1,0:T(8,128)(2,1)S(1)}) custom-call(f32[192,1152]{1,0:T(8,128)S(1)} %get-tuple-element.24.refs_0_, f32[192,1152]{1,0:T(8,128)S(1)} %shard_map.167.refs_1_, bf16[192,1152]{1,0:T(8,128)(2,1)S(1)} %collective-permute-done.4.refs_2_, bf16[1152]{0:T(1024)(128)(2,1)} %refs_3_.7, f32[1152]{0:T(1024)} %refs_4_.7, ...), custom_call_target="tpu_custom_call" | custom-call | flops 28311552 | tf_op jit(solution)/shard_map/pallas_call | solution.py:286
  41.8 0.7 collective-permute-start.5
  42.5 1.5 %collective-permute-start.7 = (bf16[136,1152]{1,0:T(8,128)(2,1)S(1)}, bf16[136,1152]{1,0:T(8,128)(2,1)S(1)}, u32[]{:S(2)}, u32[]{:S(2)}) collective-permute-start(bf16[136,1152]{1,0:T(8,128)(2,1)S(1)} %collective-permute-done.2.refs_4_), channel_id=1, source_target_pairs={{0,8},{4,12},{8,0},{12,4},{1,9},{5,13},{9,1},{13,5},{2,10},{6,14},... | collective-permute-start | bytes 940040 | tf_op jit(solution)/shard_map/ppermute | solution.py:112
  44.1 0.5 collective-permute-start.6
  44.6 1.4 %collective-permute-start.8 = (bf16[136,1152]{1,0:T(8,128)(2,1)S(1)}, bf16[136,1152]{1,0:T(8,128)(2,1)S(1)}, u32[]{:S(2)}, u32[]{:S(2)}) collective-permute-start(bf16[136,1152]{1,0:T(8,128)(2,1)S(1)} %collective-permute-done.2.refs_4_), channel_id=1, source_target_pairs={{0,24},{4,28},{8,16},{12,20},{16,8},{20,12},{24,0},{28,4},{1,25},{... | collective-permute-start | bytes 940040 | tf_op jit(solution)/shard_map/ppermute | solution.py:112
  46.0 0.0 collective-permute-done.13.refs_12_
  46.0 1.5 %collective-permute-start.16 = (bf16[136,1152]{1,0:T(8,128)(2,1)S(1)}, bf16[136,1152]{1,0:T(8,128)(2,1)S(1)}, u32[]{:S(2)}, u32[]{:S(2)}) collective-permute-start(bf16[136,1152]{1,0:T(8,128)(2,1)S(1)} %collective-permute-done.13.refs_12_), channel_id=1, source_target_pairs={{0,24},{4,28},{8,16},{12,20},{16,8},{20,12},{24,0},{28,4},{1,25},{... | collective-permute-start | bytes 940040 | tf_op jit(solution)/shard_map/ppermute | solution.py:112
  47.5 4.4 %collective-permute-done.7.refs_6_ = bf16[136,1152]{1,0:T(8,128)(2,1)S(1)} collective-permute-done((bf16[136,1152]{1,0:T(8,128)(2,1)S(1)}, bf16[136,1152]{1,0:T(8,128)(2,1)S(1)}, u32[]{:S(2)}, u32[]{:S(2)}) %collective-permute-start.7) | collective-permute-done | bytes 313376 | tf_op jit(solution)/shard_map/ppermute | solution.py:112
  51.9 1.5 %collective-permute-start.15 = (bf16[136,1152]{1,0:T(8,128)(2,1)S(1)}, bf16[136,1152]{1,0:T(8,128)(2,1)S(1)}, u32[]{:S(2)}, u32[]{:S(2)}) collective-permute-start(bf16[136,1152]{1,0:T(8,128)(2,1)S(1)} %collective-permute-done.13.refs_12_), channel_id=1, source_target_pairs={{0,8},{4,12},{8,0},{12,4},{1,9},{5,13},{9,1},{13,5},{2,10},{6,14},... | collective-permute-start | bytes 940040 | tf_op jit(solution)/shard_map/ppermute | solution.py:112
  53.4 0.9 collective-permute-done.6.refs_5_
  54.3 0.5 collective-permute-start.14
  54.9 6.2 %collective-permute-done.8.refs_7_ = bf16[136,1152]{1,0:T(8,128)(2,1)S(1)} collective-permute-done((bf16[136,1152]{1,0:T(8,128)(2,1)S(1)}, bf16[136,1152]{1,0:T(8,128)(2,1)S(1)}, u32[]{:S(2)}, u32[]{:S(2)}) %collective-permute-start.8) | collective-permute-done | bytes 313376 | tf_op jit(solution)/shard_map/ppermute | solution.py:112
  61.1 0.0 collective-permute-start.9
  61.1 6.7 %collective-permute-done.16.refs_15_ = bf16[136,1152]{1,0:T(8,128)(2,1)S(1)} collective-permute-done((bf16[136,1152]{1,0:T(8,128)(2,1)S(1)}, bf16[136,1152]{1,0:T(8,128)(2,1)S(1)}, u32[]{:S(2)}, u32[]{:S(2)}) %collective-permute-start.16) | collective-permute-done | bytes 313376 | tf_op jit(solution)/shard_map/ppermute | solution.py:112
  67.7 0.0 collective-permute-start.10
  67.7 0.0 collective-permute-done.5.refs_0_.refs_1_
  67.7 0.5 collective-permute-start.11
  68.2 4.0 %collective-permute-done.15.refs_14_ = bf16[136,1152]{1,0:T(8,128)(2,1)S(1)} collective-permute-done((bf16[136,1152]{1,0:T(8,128)(2,1)S(1)}, bf16[136,1152]{1,0:T(8,128)(2,1)S(1)}, u32[]{:S(2)}, u32[]{:S(2)}) %collective-permute-start.15) | collective-permute-done | bytes 313376 | tf_op jit(solution)/shard_map/ppermute | solution.py:112
  72.2 0.0 collective-permute-start.12
  72.2 0.8 collective-permute-done.14.refs_13_
  73.0 0.0 collective-permute-start.17
  73.0 0.0 collective-permute-done.9.refs_8_
  73.0 0.5 collective-permute-start.18
  73.5 0.0 collective-permute-done.10.refs_9_
  73.5 0.1 collective-permute-start.19
  73.6 0.0 collective-permute-done.11.refs_10_
  73.6 0.4 collective-permute-start.20
  74.0 2.2 %shard_map.169.refs_3_ = f32[192,1152]{1,0:T(8,128)S(1)} custom-call(bf16[192,1152]{1,0:T(8,128)(2,1)S(1)} %collective-permute-done.5.refs_0_.refs_1_, bf16[1076,1152]{1,0:T(8,128)(2,1)S(1)} %bitcast.9, bf16[1076]{0:T(1024)(128)(2,1)S(1)} %copy-done.5, bf16[1076,1152]{1,0:T(8,128)(2,1)S(1)} %copy-done.3), custom_call_target="tpu_custom_call" | custom-call | flops 951975936 | tf_op jit(solution)/shard_map/pallas_call | solution.py:286
  76.2 0.0 collective-permute-done.12.refs_11_
  76.3 0.0 collective-permute-done.17.refs_16_
  76.3 0.0 collective-permute-done.18.refs_17_
  76.3 0.0 collective-permute-done.19.refs_18_
  76.3 0.0 collective-permute-done.20.refs_19_
  76.3 2.6 %shard_map.170 = bf16[192,1152]{1,0:T(8,128)(2,1)S(1)} custom-call(s32[1]{0:T(128)} %bitcast.refs_0_, bf16[192,1152]{1,0:T(8,128)(2,1)S(1)} %collective-permute-done.5.refs_0_.refs_1_, bf16[1076]{0:T(1024)(128)(2,1)S(1)} %collective-permute-done.3.refs_2_, f32[192,1152]{1,0:T(8,128)S(1)} %shard_map.169.refs_3_, ...), custom_call_target="tpu_custom_call" | custom-call | flops 951975936 | tf_op jit(solution)/shard_map/pallas_call | solution.py:286
  78.9 0.0 copy-start.6
  79.0 0.4 collective-permute-start.21
  79.4 2.2 %shard_map.171.refs_3_ = f32[192,1152]{1,0:T(8,128)S(1)} custom-call(bf16[192,1152]{1,0:T(8,128)(2,1)S(1)} %get-tuple-element.41.refs_0_.refs_1_, bf16[1076,1152]{1,0:T(8,128)(2,1)S(1)} %bitcast.10, bf16[1076]{0:T(1024)(128)(2,1)S(1)} %copy-done.5, bf16[1076,1152]{1,0:T(8,128)(2,1)S(1)} %copy-done.3), custom_call_target="tpu_custom_call" | custom-call | flops 951975936 | tf_op jit(solution)/shard_map/pallas_call | solution.py:286
  81.6 2.5 %shard_map.172 = f32[192,1152]{1,0:T(8,128)S(1)} custom-call(s32[1]{0:T(128)} %bitcast.refs_0_, bf16[192,1152]{1,0:T(8,128)(2,1)S(1)} %get-tuple-element.41.refs_0_.refs_1_, bf16[1076]{0:T(1024)(128)(2,1)S(1)} %collective-permute-done.3.refs_2_, f32[192,1152]{1,0:T(8,128)S(1)} %shard_map.171.refs_3_, bf16[136,1152]{1,0:T(8,128)(2,1)S(1)} %collective-permute-done.2.refs_4_, ...), custom_call_target="tpu_custom_call" | custom-call | flops 951975936 | tf_op jit(solution)/shard_map/pallas_call | solution.py:286
  84.1 7.1 %collective-permute-done.21 = bf16[192,1152]{1,0:T(8,128)(2,1)S(1)} collective-permute-done((bf16[192,1152]{1,0:T(8,128)(2,1)S(1)}, bf16[192,1152]{1,0:T(8,128)(2,1)S(1)}, u32[]{:S(2)}, u32[]{:S(2)}) %collective-permute-start.21) | collective-permute-done | bytes 442400 | tf_op jit(solution)/shard_map/ppermute | solution.py:112
  91.2 0.9 fusion
  (10 shorter events, 0.0 us)
Async XLA Ops:
  1.8 13.2 %collective-permute-start = (bf16[192,1152]{1,0:T(8,128)(2,1)S(1)}, bf16[192,1152]{1,0:T(8,128)(2,1)S(1)}, u32[]{:S(2)}, u32[]{:S(2)}) collective-permute-start(bf16[192,1152]{1,0:T(8,128)(2,1)S(1)} %get-tuple-element.27.refs_0_), channel_id=1, source_target_pairs={{0,16},{16,0},{1,17},{17,1},{2,18},{18,2},{3,19},{19,3},{4,20},{20... | collective-permute-start | bytes 1327112 | tf_op jit(solution)/shard_map/ppermute | solution.py:112
  4.9 11.6 %collective-permute-start.1 = (s32[1,192]{1,0:T(1,128)}, s32[1,192]{1,0:T(1,128)S(1)}, u32[]{:S(2)}, u32[]{:S(2)}) collective-permute-start(s32[1,192]{1,0:T(1,128)} %refs_2_.5), channel_id=1, source_target_pairs={{0,16},{16,0},{1,17},{17,1},{2,18},{18,2},{3,19},{19,3},{4,20},{20... | collective-permute-start | bytes 2312 | tf_op jit(solution)/shard_map/ppermute | solution.py:112
  6.0 31.4 %collective-permute-start.2 = (bf16[136,1152]{1,0:T(8,128)(2,1)S(1)}, bf16[136,1152]{1,0:T(8,128)(2,1)S(1)}, u32[]{:S(2)}, u32[]{:S(2)}) collective-permute-start(bf16[136,1152]{1,0:T(8,128)(2,1)S(1)} %constant_dynamic-slice_fusion), channel_id=1, source_target_pairs={{0,2},{1,3},{2,0},{3,1},{4,6},{5,7},{6,4},{7,5},{8,10},{9,11},{10,... | collective-permute-start | bytes 940040 | tf_op jit(solution)/shard_map/ppermute | solution.py:112
  9.1 2.1 %copy-start = (bf16[1152,1728]{0,1:T(8,128)(2,1)S(1)}, bf16[1152,1728]{0,1:T(8,128)(2,1)}, u32[]{:S(2)}) copy-start(bf16[1152,1728]{0,1:T(8,128)(2,1)} %param.25) | copy-start | bytes 11943940
  11.2 3.8 %copy-start.1 = (bf16[1152,1728]{0,1:T(8,128)(2,1)S(1)}, bf16[1152,1728]{0,1:T(8,128)(2,1)}, u32[]{:S(2)}) copy-start(bf16[1152,1728]{0,1:T(8,128)(2,1)} %param.25) | copy-start | bytes 11943940
  12.6 3.8 %copy-start.4 = (bf16[576,1152]{1,0:T(8,128)(2,1)S(1)}, bf16[576,1152]{1,0:T(8,128)(2,1)}, u32[]{:S(2)}) copy-start(bf16[576,1152]{1,0:T(8,128)(2,1)} %refs_4_.6) | copy-start | bytes 3981316
  12.6 3.8 %copy-start.7 = (s32[1,192]{1,0:T(1,128)S(1)}, s32[1,192]{1,0:T(1,128)}, u32[]{:S(2)}) copy-start(s32[1,192]{1,0:T(1,128)} %refs_2_.5) | copy-start | bytes 2308
  16.4 5.0 %copy-start.3 = (bf16[1076,1152]{1,0:T(8,128)(2,1)S(1)}, bf16[1076,1152]{1,0:T(8,128)(2,1)}, u32[]{:S(2)}) copy-start(bf16[1076,1152]{1,0:T(8,128)(2,1)} %refs_3_.9) | copy-start | bytes 7437316
  16.4 7.8 %copy-start.5 = (bf16[1076]{0:T(1024)(128)(2,1)S(1)}, bf16[1076]{0:T(1024)(128)(2,1)}, u32[]{:S(2)}) copy-start(bf16[1076]{0:T(1024)(128)(2,1)} %refs_2_.7) | copy-start | bytes 6460
  19.6 21.0 %collective-permute-start.4 = (bf16[192,1152]{1,0:T(8,128)(2,1)S(1)}, bf16[192,1152]{1,0:T(8,128)(2,1)S(1)}, u32[]{:S(2)}, u32[]{:S(2)}) collective-permute-start(bf16[192,1152]{1,0:T(8,128)(2,1)S(1)} %shard_map.166), channel_id=1, source_target_pairs={{0,16},{16,0},{1,17},{17,1},{2,18},{18,2},{3,19},{19,3},{4,20},{20... | collective-permute-start | bytes 1327112 | tf_op jit(solution)/shard_map/ppermute | solution.py:112
  21.5 52.5 %copy-start.2 = (bf16[1152,1076]{0,1:T(8,128)(2,1)S(1)}, bf16[1152,1076]{0,1:T(8,128)(2,1)}, u32[]{:S(2)}) copy-start(bf16[1152,1076]{0,1:T(8,128)(2,1)} %param.30) | copy-start | bytes 7437316
  21.6 24.5 %collective-permute-start.13 = (bf16[136,1152]{1,0:T(8,128)(2,1)S(1)}, bf16[136,1152]{1,0:T(8,128)(2,1)S(1)}, u32[]{:S(2)}, u32[]{:S(2)}) collective-permute-start(bf16[136,1152]{1,0:T(8,128)(2,1)S(1)} %dynamic-slice_select_fusion), channel_id=1, source_target_pairs={{0,2},{1,3},{2,0},{3,1},{4,6},{5,7},{6,4},{7,5},{8,10},{9,11},{10,... | collective-permute-start | bytes 940040 | tf_op jit(solution)/shard_map/ppermute | solution.py:112
  24.2 13.2 %collective-permute-start.3 = (bf16[1076]{0:T(1024)(128)(2,1)S(1)}, bf16[1076]{0:T(1024)(128)(2,1)S(1)}, u32[]{:S(2)}, u32[]{:S(2)}) collective-permute-start(bf16[1076]{0:T(1024)(128)(2,1)S(1)} %copy-done.5), channel_id=1, source_target_pairs={{0,2},{1,3},{2,0},{3,1},{4,6},{5,7},{6,4},{7,5},{8,10},{9,11},{10,... | collective-permute-start | bytes 6464 | tf_op jit(solution)/shard_map/ppermute | solution.py:112
  41.8 26.0 %collective-permute-start.5 = (bf16[192,1152]{1,0:T(8,128)(2,1)S(1)}, bf16[192,1152]{1,0:T(8,128)(2,1)S(1)}, u32[]{:S(2)}, u32[]{:S(2)}) collective-permute-start(bf16[192,1152]{1,0:T(8,128)(2,1)S(1)} %get-tuple-element.41.refs_0_.refs_1_), channel_id=1, source_target_pairs={{0,1},{1,0},{2,3},{3,2},{4,5},{5,4},{6,7},{7,6},{8,9},{9,8},{10,11... | collective-permute-start | bytes 1327112 | tf_op jit(solution)/shard_map/ppermute | solution.py:112
  42.5 9.4 %collective-permute-start.7 = (bf16[136,1152]{1,0:T(8,128)(2,1)S(1)}, bf16[136,1152]{1,0:T(8,128)(2,1)S(1)}, u32[]{:S(2)}, u32[]{:S(2)}) collective-permute-start(bf16[136,1152]{1,0:T(8,128)(2,1)S(1)} %collective-permute-done.2.refs_4_), channel_id=1, source_target_pairs={{0,8},{4,12},{8,0},{12,4},{1,9},{5,13},{9,1},{13,5},{2,10},{6,14},... | collective-permute-start | bytes 940040 | tf_op jit(solution)/shard_map/ppermute | solution.py:112
  44.1 10.3 %collective-permute-start.6 = (bf16[136,1152]{1,0:T(8,128)(2,1)S(1)}, bf16[136,1152]{1,0:T(8,128)(2,1)S(1)}, u32[]{:S(2)}, u32[]{:S(2)}) collective-permute-start(bf16[136,1152]{1,0:T(8,128)(2,1)S(1)} %collective-permute-done.2.refs_4_), channel_id=1, source_target_pairs={{0,16},{16,0},{1,17},{17,1},{2,18},{18,2},{3,19},{19,3},{4,20},{20... | collective-permute-start | bytes 940040 | tf_op jit(solution)/shard_map/ppermute | solution.py:112
  44.6 16.5 %collective-permute-start.8 = (bf16[136,1152]{1,0:T(8,128)(2,1)S(1)}, bf16[136,1152]{1,0:T(8,128)(2,1)S(1)}, u32[]{:S(2)}, u32[]{:S(2)}) collective-permute-start(bf16[136,1152]{1,0:T(8,128)(2,1)S(1)} %collective-permute-done.2.refs_4_), channel_id=1, source_target_pairs={{0,24},{4,28},{8,16},{12,20},{16,8},{20,12},{24,0},{28,4},{1,25},{... | collective-permute-start | bytes 940040 | tf_op jit(solution)/shard_map/ppermute | solution.py:112
  46.0 21.7 %collective-permute-start.16 = (bf16[136,1152]{1,0:T(8,128)(2,1)S(1)}, bf16[136,1152]{1,0:T(8,128)(2,1)S(1)}, u32[]{:S(2)}, u32[]{:S(2)}) collective-permute-start(bf16[136,1152]{1,0:T(8,128)(2,1)S(1)} %collective-permute-done.13.refs_12_), channel_id=1, source_target_pairs={{0,24},{4,28},{8,16},{12,20},{16,8},{20,12},{24,0},{28,4},{1,25},{... | collective-permute-start | bytes 940040 | tf_op jit(solution)/shard_map/ppermute | solution.py:112
  51.9 20.3 %collective-permute-start.15 = (bf16[136,1152]{1,0:T(8,128)(2,1)S(1)}, bf16[136,1152]{1,0:T(8,128)(2,1)S(1)}, u32[]{:S(2)}, u32[]{:S(2)}) collective-permute-start(bf16[136,1152]{1,0:T(8,128)(2,1)S(1)} %collective-permute-done.13.refs_12_), channel_id=1, source_target_pairs={{0,8},{4,12},{8,0},{12,4},{1,9},{5,13},{9,1},{13,5},{2,10},{6,14},... | collective-permute-start | bytes 940040 | tf_op jit(solution)/shard_map/ppermute | solution.py:112
  54.3 18.6 %collective-permute-start.14 = (bf16[136,1152]{1,0:T(8,128)(2,1)S(1)}, bf16[136,1152]{1,0:T(8,128)(2,1)S(1)}, u32[]{:S(2)}, u32[]{:S(2)}) collective-permute-start(bf16[136,1152]{1,0:T(8,128)(2,1)S(1)} %collective-permute-done.13.refs_12_), channel_id=1, source_target_pairs={{0,16},{16,0},{1,17},{17,1},{2,18},{18,2},{3,19},{19,3},{4,20},{20... | collective-permute-start | bytes 940040 | tf_op jit(solution)/shard_map/ppermute | solution.py:112
  61.1 11.9 %collective-permute-start.9 = (bf16[136,1152]{1,0:T(8,128)(2,1)S(1)}, bf16[136,1152]{1,0:T(8,128)(2,1)S(1)}, u32[]{:S(2)}, u32[]{:S(2)}) collective-permute-start(bf16[136,1152]{1,0:T(8,128)(2,1)S(1)} %collective-permute-done.2.refs_4_), channel_id=1, source_target_pairs={{0,4},{4,0},{8,12},{12,8},{1,5},{5,1},{9,13},{13,9},{2,6},{6,2},{1... | collective-permute-start | bytes 940040 | tf_op jit(solution)/shard_map/ppermute | solution.py:112
  67.7 5.8 %collective-permute-start.10 = (bf16[136,1152]{1,0:T(8,128)(2,1)S(1)}, bf16[136,1152]{1,0:T(8,128)(2,1)S(1)}, u32[]{:S(2)}, u32[]{:S(2)}) collective-permute-start(bf16[136,1152]{1,0:T(8,128)(2,1)S(1)} %collective-permute-done.6.refs_5_), channel_id=1, source_target_pairs={{0,4},{4,0},{8,12},{12,8},{1,5},{5,1},{9,13},{13,9},{2,6},{6,2},{1... | collective-permute-start | bytes 940040 | tf_op jit(solution)/shard_map/ppermute | solution.py:112
  67.7 5.8 %collective-permute-start.11 = (bf16[136,1152]{1,0:T(8,128)(2,1)S(1)}, bf16[136,1152]{1,0:T(8,128)(2,1)S(1)}, u32[]{:S(2)}, u32[]{:S(2)}) collective-permute-start(bf16[136,1152]{1,0:T(8,128)(2,1)S(1)} %collective-permute-done.7.refs_6_), channel_id=1, source_target_pairs={{0,4},{4,0},{8,12},{12,8},{1,5},{5,1},{9,13},{13,9},{2,6},{6,2},{1... | collective-permute-start | bytes 940040 | tf_op jit(solution)/shard_map/ppermute | solution.py:112
  72.2 4.0 %collective-permute-start.12 = (bf16[136,1152]{1,0:T(8,128)(2,1)S(1)}, bf16[136,1152]{1,0:T(8,128)(2,1)S(1)}, u32[]{:S(2)}, u32[]{:S(2)}) collective-permute-start(bf16[136,1152]{1,0:T(8,128)(2,1)S(1)} %collective-permute-done.8.refs_7_), channel_id=1, source_target_pairs={{0,4},{4,0},{8,12},{12,8},{1,5},{5,1},{9,13},{13,9},{2,6},{6,2},{1... | collective-permute-start | bytes 940040 | tf_op jit(solution)/shard_map/ppermute | solution.py:112
  73.0 3.3 %collective-permute-start.17 = (bf16[136,1152]{1,0:T(8,128)(2,1)S(1)}, bf16[136,1152]{1,0:T(8,128)(2,1)S(1)}, u32[]{:S(2)}, u32[]{:S(2)}) collective-permute-start(bf16[136,1152]{1,0:T(8,128)(2,1)S(1)} %collective-permute-done.13.refs_12_), channel_id=1, source_target_pairs={{0,4},{4,0},{8,12},{12,8},{1,5},{5,1},{9,13},{13,9},{2,6},{6,2},{1... | collective-permute-start | bytes 940040 | tf_op jit(solution)/shard_map/ppermute | solution.py:112
  73.0 3.3 %collective-permute-start.18 = (bf16[136,1152]{1,0:T(8,128)(2,1)S(1)}, bf16[136,1152]{1,0:T(8,128)(2,1)S(1)}, u32[]{:S(2)}, u32[]{:S(2)}) collective-permute-start(bf16[136,1152]{1,0:T(8,128)(2,1)S(1)} %collective-permute-done.14.refs_13_), channel_id=1, source_target_pairs={{0,4},{4,0},{8,12},{12,8},{1,5},{5,1},{9,13},{13,9},{2,6},{6,2},{1... | collective-permute-start | bytes 940040 | tf_op jit(solution)/shard_map/ppermute | solution.py:112
  73.5 2.8 %collective-permute-start.19 = (bf16[136,1152]{1,0:T(8,128)(2,1)S(1)}, bf16[136,1152]{1,0:T(8,128)(2,1)S(1)}, u32[]{:S(2)}, u32[]{:S(2)}) collective-permute-start(bf16[136,1152]{1,0:T(8,128)(2,1)S(1)} %collective-permute-done.15.refs_14_), channel_id=1, source_target_pairs={{0,4},{4,0},{8,12},{12,8},{1,5},{5,1},{9,13},{13,9},{2,6},{6,2},{1... | collective-permute-start | bytes 940040 | tf_op jit(solution)/shard_map/ppermute | solution.py:112
  73.6 2.7 %collective-permute-start.20 = (bf16[136,1152]{1,0:T(8,128)(2,1)S(1)}, bf16[136,1152]{1,0:T(8,128)(2,1)S(1)}, u32[]{:S(2)}, u32[]{:S(2)}) collective-permute-start(bf16[136,1152]{1,0:T(8,128)(2,1)S(1)} %collective-permute-done.16.refs_15_), channel_id=1, source_target_pairs={{0,4},{4,0},{8,12},{12,8},{1,5},{5,1},{9,13},{13,9},{2,6},{6,2},{1... | collective-permute-start | bytes 940040 | tf_op jit(solution)/shard_map/ppermute | solution.py:112
  78.9 2.7 %copy-start.6 = (bf16[1152]{0:T(1024)(128)(2,1)S(1)}, bf16[1152]{0:T(1024)(128)(2,1)}, u32[]{:S(2)}) copy-start(bf16[1152]{0:T(1024)(128)(2,1)} %refs_21_.1) | copy-start | bytes 6916
  79.0 12.2 %collective-permute-start.21 = (bf16[192,1152]{1,0:T(8,128)(2,1)S(1)}, bf16[192,1152]{1,0:T(8,128)(2,1)S(1)}, u32[]{:S(2)}, u32[]{:S(2)}) collective-permute-start(bf16[192,1152]{1,0:T(8,128)(2,1)S(1)} %shard_map.170), channel_id=1, source_target_pairs={{0,1},{1,0},{2,3},{3,2},{4,5},{5,4},{6,7},{7,6},{8,9},{9,8},{10,11... | collective-permute-start | bytes 1327112 | tf_op jit(solution)/shard_map/ppermute | solution.py:112

commit v2 on v1

--- a/solution.py
+++ b/solution.py
@@ -135,21 +135,19 @@
     return moved * lax.rsqrt(spread + 1e-06) * gain + shift
 
 
-def embed_kernel(patch, rows, cols, row_tab, col_tab, gain, shift, embedded, normed):
+def project_kernel(patch, places, row_tab, col_tab, gain, shift, weight, out, *embedded):
     tokens = patch.shape[0]
     grid = row_tab.shape[0]
     level = lax.broadcasted_iota(jnp.int32, (grid, tokens), 0)
-    hot = jnp.concatenate([level == rows[...], level == cols[...]], 0)
+    hot = jnp.concatenate([level == places[0:1, :], level == places[1:2, :]], 0)
     hot = jnp.where(hot, 1.0, 0.0).astype(jnp.bfloat16)
     table = jnp.concatenate([row_tab[...], col_tab[...]], 0)
     values = patch[...].astype(jnp.float32) + tn_dot(hot, table)
-    embedded[...] = values
-    normed[...] = norm_rows(values, gain[...][None], shift[...][None]).astype(jnp.bfloat16)
-
-
-def qkv_kernel(normed, weight, out):
+    for ref in embedded:
+        ref[...] = values
+    normed = norm_rows(values, gain[...][None], shift[...][None]).astype(jnp.bfloat16)
     head_dim = out.shape[1]
-    product = dot_t(weight[...], normed[...])
+    product = dot_t(weight[...], normed)
     for part in range(out.shape[0]):
         out[part] = product[part * head_dim : (part + 1) * head_dim].astype(jnp.bfloat16)
 
@@ -161,12 +159,12 @@
     return jnp.sum(jnp.where(across == along, row, 0.0), -1, keepdims=True)
 
 
-def attend_kernel(near, far, seg_near, seg_far, weight, out, mixed):
+def attend_kernel(near, far, near_places, far_places, weight, out, mixed):
     head_dim = near.shape[1]
     heads = near.shape[0] // 3
     scale = math.log2(math.e) / math.sqrt(head_dim)
-    asked = seg_near[...].astype(jnp.float32)
-    same = [column_of(seg[...].astype(jnp.float32)) == asked for seg in (seg_near, seg_far)]
+    segs = [places[2:3, :].astype(jnp.float32) for places in (near_places, far_places)]
+    same = [column_of(seg) == segs[0] for seg in segs]
     for head in range(heads):
         query = near[3 * head]
         scores = []
@@ -212,9 +210,9 @@
             total[...] += piece
 
 
-def far_mlp_kernel(count, place, inputs, bias, total, *refs):
-    ups, downs = refs[:count], refs[count : 2 * count]
-    rest = refs[2 * count :]
+def far_mlp_kernel(count, extra, place, inputs, bias, total, *refs):
+    ups, downs = refs[:count], refs[count : 2 * count + extra]
+    rest = refs[2 * count + extra :]
     rows = ups[0].shape[0]
     hidden = bias.shape[0]
     line = bias[...].astype(jnp.float32)[None]
@@ -229,9 +227,11 @@
         bit *= 2
     order = [step ^ core for core in (0, 1) for step in spread_order(count)]
     up, down = rest[-2:]
-    for i in range(count):
-        up[i * rows : (i + 1) * rows, :] = ups[i][...]
-        down[i * rows : (i + 1) * rows, :] = downs[i][...]
+    for pieces, whole in ((ups, up), (downs, down)):
+        begin = 0
+        for piece in pieces:
+            whole[begin : begin + piece.shape[0], :] = piece[...]
+            begin += piece.shape[0]
     result = total[...]
     group = count // 2
     for half in range(2):
@@ -369,65 +369,62 @@
         qkv_rows = w_qkv.T
         each = 2 * tokens * width
 
-        embedded, normed = run(
-            embed_kernel,
-            8,
-            (pltpu.VMEM(block, f32), sent_block),
-            fetched=tuple(range(7)),
-            flops=each * 256,
-        )(patches[0], pos_rows, pos_cols, row_table, col_table, ln1_gain, ln1_bias)
-        normed_other = swap(normed, "seq", seq, 1)
-        seg_other = swap(seg_ids, "seq", seq, 1)
+        places = jnp.concatenate([pos_rows, pos_cols, seg_ids])
+        patches_other = swap(patches[0], "seq", seq, 1)
+        places_other = swap(places, "seq", seq, 1)
 
         rows = -(-hidden // (8 * holders)) * 8
         overlap = rows * holders - hidden
         begin = jnp.minimum(place * rows, hidden - rows)
-        share1 = lax.dynamic_slice(after(fc1_rows, normed), (begin, 0), (rows, width))
+        share1 = lax.dynamic_slice(fc1_rows, (begin, 0), (rows, width))
         far1 = swap(share1, "tp", tp, 2)
+        far_bias = swap(fc1_bias, "tp", tp, 2)
+
+        def project(values, where, fetched, *more):
+            qkv_shape = pltpu.VMEM((3 * heads_here, head_dim, tokens), bf16)
+            return run(
+                project_kernel,
+                8,
+                (qkv_shape,) + more,
+                fetched=fetched,
+                flops=each * (qkv_rows.shape[0] + 256),
+            )(values, where, row_table, col_table, ln1_gain, ln1_bias, qkv_rows)
+
+        qkv_own, embedded = project(
+            after(patches[0], share1), places, (0, 2, 3, 4, 5), pltpu.VMEM(block, f32)
+        )
         share2 = lax.dynamic_slice(after(w_fc2, share1), (begin, 0), (rows, width))
         repeated = (place == holders - 1) & (jnp.arange(rows) < overlap)
         share2 = jnp.where(repeated[:, None], jnp.zeros_like(share2), share2)
-        far2 = swap(share2, "tp", tp, 2)
-        far_bias = swap(fc1_bias, "tp", tp, 2)
-
-        def project(values):
-            return run(
-                qkv_kernel,
-                8,
-                pltpu.VMEM((3 * heads_here, head_dim, tokens), bf16),
-                flops=each * qkv_rows.shape[0],
-            )(values, qkv_rows)
-
-        qkv_own = project(after(normed, share1))
-        qkv_other = project(normed_other)
+        (qkv_other,) = project(after(patches_other, qkv_own, share2), places_other, ())
 
         def spread(share):
             along_x = swap(share, "seq", seq, 1)
             along_y = swap(share, "dp", dp, 2)
-            both = swap(share, ("seq", "dp"), seq * dp, dp + 2)
-            return [share, along_x, along_y, both]
+            return [share, along_x, along_y]
 
         def cross(shares):
             return shares + [swap(share, "dp", dp, 1) for share in shares]
 
-        def attend(near, far, seg_near, seg_far, shape):
+        def attend(near, far, near_places, far_places, shape):
             scratch = [pltpu.VMEM((heads_here * head_dim, tokens), f32)]
             return run(attend_kernel, 8, shape, scratch, flops=each * 2304)(
-                near, far, seg_near, seg_far, w_out
+                near, far, near_places, far_places, w_out
             )
 
-        sent = attend(qkv_other, qkv_own, seg_other, seg_ids, sent_block)
+        sent = attend(qkv_other, qkv_own, places_other, places, sent_block)
         got = swap(sent, "seq", seq, 1)
+        far2 = swap(after(share2, sent), "tp", tp, 2)
         near1 = spread(after(far1, sent))
-        kept = attend(
-            after(qkv_own, sent, far1, far_bias), qkv_other, seg_ids, seg_other, pltpu.VMEM(block, f32)
-        )
+        kept = attend(after(qkv_own, sent), qkv_other, places, places_other, pltpu.VMEM(block, f32))
         attended, normed2 = run(
             join_kernel, 8, (pltpu.VMEM(block, f32), sent_block), fetched=(3, 4, 5), flops=each * 64
         )(embedded, kept, got, out_bias, ln2_gain, ln2_bias)
         partner = swap(normed2, "tp", tp, 1)
+        near1 = near1 + [swap(after(near1[1], normed2), "dp", dp, 2)]
         ups = cross([after(share, normed2) for share in near1])
         near2 = spread(after(far2, normed2))
+        near2 = near2 + [swap(near2[2], "seq", seq, 1)]
 
         def mlp(values):
             return run(
@@ -440,7 +437,7 @@
 
         def far_mlp(values, total, shape, *tail):
             return run(
-                functools.partial(far_mlp_kernel, holders),
+                functools.partial(far_mlp_kernel, holders, len(downs) - holders),
                 14,
                 shape,
                 [pltpu.VMEM((holders * rows, width), bf16)] * 2,

time: 92.3 us -> 86 us (0.932)
  waiting for transfers between devices: 45.3 us -> 40.2 us
  starting transfers between devices: 20.8 us -> 17.1 us
  other arithmetic: 0.99 us -> 2.68 us
    ppermute x22, waiting for transfers between devices: 45.3 us -> 40.2 us  [swap(): return lax.ppermute(values, axis, [(i, i ^ bit) for i in range(size)])]
    ppermute x22, starting transfers between devices: 20.8 us -> 17.1 us  [swap(): return lax.ppermute(values, axis, [(i, i ^ bit) for i in range(size)])]
    select_n x1, other arithmetic: 0.12 us -> 1.09 us  [steps(): share2 = jnp.where(repeated[:, None], jnp.zeros_like(share2), share2)]
    pallas_call x10 -> x9, Pallas kernels: 21.5 us -> 22.2 us  [call(): pl.pallas_call(body, in_specs=specs, out_shape=out_shape, scratch_shapes=...]
    unnamed x16 -> x22, local copies, waits for them, and re-layouts: 2.17 us -> 2.17 us
  transfers between devices with their start and end apart: 22 -> 22, of which waited for: 9 -> 8; matrix products, arithmetic and copies ran while one was open for 1% -> 3% of each run, Pallas kernels for 19% -> 23%
where the time goes in v2:
time: 86 us; the launch traced here: 85.7 us
  waiting for transfers between devices  40.2 us (47%)
  Pallas kernels  22.2 us (26%)
  starting transfers between devices  17.1 us (20%)
  local copies, waits for them, and re-layouts  3.22 us (4%)
  other arithmetic  2.68 us (3%)
    ppermute x22, waiting for transfers between devices, swap(): return lax.ppermute(values, axis, [(i, i ^ bit) for i in range(size)])  40.2 us
    pallas_call x9, Pallas kernels, call(): pl.pallas_call(body, in_specs=specs, out_shape=out_shape, scratch_shapes=...  22.2 us
    ppermute x22, starting transfers between devices, swap(): return lax.ppermute(values, axis, [(i, i ^ bit) for i in range(size)])  17.1 us
    unnamed x22, local copies, waits for them, and re-layouts  2.17 us
  transfers between devices with their start and end apart: 22, of which 8 were waited for; matrix products, arithmetic and copies ran while one was open for 3% of the time, Pallas kernels for 23%

profile of v2, /device:TPU:0, one launch (start us, length us, event | category | flops | bytes accessed | tf_op | source)
XLA Modules:
  0.0 85.7 jit_solution(6001926915453888721)
XLA Ops:
  0.0 0.7 pad_add_fusion.refs_1_.refs_3_.refs_2_
  0.7 3.0 %collective-permute-start.1 = (s32[3,192]{1,0:T(4,128)S(1)}, s32[3,192]{1,0:T(4,128)S(1)}, u32[]{:S(2)}, u32[]{:S(2)}) collective-permute-start(s32[3,192]{1,0:T(4,128)S(1)} %pad_add_fusion.refs_1_.refs_3_.refs_2_), channel_id=1, source_target_pairs={{0,16},{16,0},{1,17},{17,1},{2,18},{18,2},{3,19},{19,3},{4,20},{20... | collective-permute-start | bytes 6920 | tf_op jit(solution)/shard_map/ppermute | solution.py:112
  3.7 1.1 %dynamic-slice_bitcast_fusion = bf16[136,1152]{1,0:T(8,128)(2,1)S(1)} fusion(bf16[1152,1076]{0,1:T(8,128)(2,1)} %param.30, s32[]{:T(128)S(6)} %select_n.8), kind=kLoop, calls=%fused_computation.3 | loop fusion | bytes 626692 | tf_op jit(solution)/shard_map/dynamic_slice | solution.py:379
  4.8 2.7 %collective-permute-start.5 = (bf16[136,1152]{1,0:T(8,128)(2,1)S(1)}, bf16[136,1152]{1,0:T(8,128)(2,1)S(1)}, u32[]{:S(2)}, u32[]{:S(2)}) collective-permute-start(bf16[136,1152]{1,0:T(8,128)(2,1)S(1)} %dynamic-slice_bitcast_fusion), channel_id=1, source_target_pairs={{0,2},{1,3},{2,0},{3,1},{4,6},{5,7},{6,4},{7,5},{8,10},{9,11},{10,... | collective-permute-start | bytes 940040 | tf_op jit(solution)/shard_map/ppermute | solution.py:112
  7.5 0.5 collective-permute-start
  8.0 1.1 %dynamic-slice_select_fusion = bf16[136,1152]{1,0:T(8,128)(2,1)S(1)} fusion(bf16[1076,1152]{1,0:T(8,128)(2,1)} %refs_3_.9, s32[]{:T(128)S(6)} %select_n.8, pred[136]{0:T(512)(128)(4,1)S(1)} %compare_and_fusion), kind=kLoop, calls=%fused_computation.2 | loop fusion | flops 156672 | bytes 626828 | tf_op jit(solution)/shard_map/jit(_where)/select_n | solution.py:398
  9.1 0.0 copy-start
  9.1 2.1 %copy-done = bf16[1152,1728]{0,1:T(8,128)(2,1)S(1)} copy-done((bf16[1152,1728]{0,1:T(8,128)(2,1)S(1)}, bf16[1152,1728]{0,1:T(8,128)(2,1)}, u32[]{:S(2)}) %copy-start) | copy-done | bytes 3981336
  11.2 0.0 copy-start.8
  11.2 3.2 %shard_map.163 = (bf16[24,72,192]{2,1,0:T(8,128)(2,1)S(1)}, f32[192,1152]{1,0:T(8,128)S(1)}) custom-call(bf16[192,1152]{1,0:T(8,128)(2,1)} %bitcast.13, s32[3,192]{1,0:T(4,128)S(1)} %pad_add_fusion.refs_1_.refs_3_.refs_2_, bf16[64,1152]{1,0:T(8,128)(2,1)} %refs_2_.5, bf16[64,1152]{1,0:T(8,128)(2,1)} %refs_3_.6, f32[1152]{0:T(1024)} %refs_4_.6, ...), custom_call_target="tpu_custom_call" | custom-call | flops 877658112 | tf_op jit(solution)/shard_map/pallas_call | solution.py:286
  14.5 4.5 %collective-permute-done.refs_0_ = bf16[192,1152]{1,0:T(8,128)(2,1)S(1)} collective-permute-done((bf16[192,1152]{1,0:T(8,128)(2,1)}, bf16[192,1152]{1,0:T(8,128)(2,1)S(1)}, u32[]{:S(2)}, u32[]{:S(2)}) %collective-permute-start) | collective-permute-done | bytes 442400 | tf_op jit(solution)/shard_map/ppermute | solution.py:112
  19.0 0.0 collective-permute-done.1.refs_1_.refs_2_.refs_3_
  19.1 1.9 %shard_map.164.refs_0_.refs_1_ = bf16[24,72,192]{2,1,0:T(8,128)(2,1)S(1)} custom-call(bf16[192,1152]{1,0:T(8,128)(2,1)S(1)} %collective-permute-done.refs_0_, s32[3,192]{1,0:T(4,128)S(1)} %collective-permute-done.1.refs_1_.refs_2_.refs_3_, bf16[64,1152]{1,0:T(8,128)(2,1)S(1)} %copy-done.5, bf16[64,1152]{1,0:T(8,128)(2,1)S(1)} %copy-done.6, ...), custom_call_target="tpu_custom_call" | custom-call | flops 877658112 | tf_op jit(solution)/shard_map/pallas_call | solution.py:286
  21.0 3.2 %shard_map.165 = bf16[192,1152]{1,0:T(8,128)(2,1)S(1)} custom-call(bf16[24,72,192]{2,1,0:T(8,128)(2,1)S(1)} %shard_map.164.refs_0_.refs_1_, bf16[24,72,192]{2,1,0:T(8,128)(2,1)S(1)} %get-tuple-element.30.refs_1_.refs_0_, s32[3,192]{1,0:T(4,128)S(1)} %collective-permute-done.1.refs_1_.refs_2_.refs_3_, s32[3,192]{1,0:T(4,128)S(1)} %pad_add_fusion.refs_1_.refs_3_.refs_2_, ...), custom_call_target="tpu_custom_call" | custom-call | flops 1019215872 | tf_op jit(solution)/shard_map/pallas_call | solution.py:286
  24.2 0.0 copy-start.9
  24.2 0.0 copy-start.2
  24.2 0.0 copy-start.3
  24.3 0.6 collective-permute-start.2
  24.9 0.4 collective-permute-start.13
  25.2 0.0 collective-permute-done.5.refs_4_
  25.2 1.5 %collective-permute-start.6 = (bf16[136,1152]{1,0:T(8,128)(2,1)S(1)}, bf16[136,1152]{1,0:T(8,128)(2,1)S(1)}, u32[]{:S(2)}, u32[]{:S(2)}) collective-permute-start(bf16[136,1152]{1,0:T(8,128)(2,1)S(1)} %collective-permute-done.5.refs_4_), channel_id=1, source_target_pairs={{0,16},{16,0},{1,17},{17,1},{2,18},{18,2},{3,19},{19,3},{4,20},{20... | collective-permute-start | bytes 940040 | tf_op jit(solution)/shard_map/ppermute | solution.py:112
  26.7 3.2 %shard_map.166.refs_1_ = f32[192,1152]{1,0:T(8,128)S(1)} custom-call(bf16[24,72,192]{2,1,0:T(8,128)(2,1)S(1)} %get-tuple-element.30.refs_1_.refs_0_, bf16[24,72,192]{2,1,0:T(8,128)(2,1)S(1)} %shard_map.164.refs_0_.refs_1_, s32[3,192]{1,0:T(4,128)S(1)} %pad_add_fusion.refs_1_.refs_3_.refs_2_, s32[3,192]{1,0:T(4,128)S(1)} %collective-permute-done.1.refs_1_.refs_2_.refs_3_, ...), custom_call_target="tpu_custom_call" | custom-call | flops 1019215872 | tf_op jit(solution)/shard_map/pallas_call | solution.py:286
  29.9 7.5 %collective-permute-done.2.refs_2_ = bf16[192,1152]{1,0:T(8,128)(2,1)S(1)} collective-permute-done((bf16[192,1152]{1,0:T(8,128)(2,1)S(1)}, bf16[192,1152]{1,0:T(8,128)(2,1)S(1)}, u32[]{:S(2)}, u32[]{:S(2)}) %collective-permute-start.2) | collective-permute-done | bytes 442400 | tf_op jit(solution)/shard_map/ppermute | solution.py:112
  37.4 1.2 %shard_map.167 = (f32[192,1152]{1,0:T(8,128)S(1)}, bf16[192,1152]{1,0:T(8,128)(2,1)S(1)}) custom-call(f32[192,1152]{1,0:T(8,128)S(1)} %get-tuple-element.26.refs_0_, f32[192,1152]{1,0:T(8,128)S(1)} %shard_map.166.refs_1_, bf16[192,1152]{1,0:T(8,128)(2,1)S(1)} %collective-permute-done.2.refs_2_, bf16[1152]{0:T(1024)(128)(2,1)} %refs_3_.7, f32[1152]{0:T(1024)} %refs_4_.9, ...), custom_call_target="tpu_custom_call" | custom-call | flops 28311552 | tf_op jit(solution)/shard_map/pallas_call | solution.py:286
  38.5 1.4 %collective-permute-done.13.refs_12_ = bf16[136,1152]{1,0:T(8,128)(2,1)S(1)} collective-permute-done((bf16[136,1152]{1,0:T(8,128)(2,1)S(1)}, bf16[136,1152]{1,0:T(8,128)(2,1)S(1)}, u32[]{:S(2)}, u32[]{:S(2)}) %collective-permute-start.13) | collective-permute-done | bytes 313376 | tf_op jit(solution)/shard_map/ppermute | solution.py:112
  39.9 1.5 %collective-permute-start.15 = (bf16[136,1152]{1,0:T(8,128)(2,1)S(1)}, bf16[136,1152]{1,0:T(8,128)(2,1)S(1)}, u32[]{:S(2)}, u32[]{:S(2)}) collective-permute-start(bf16[136,1152]{1,0:T(8,128)(2,1)S(1)} %collective-permute-done.13.refs_12_), channel_id=1, source_target_pairs={{0,8},{4,12},{8,0},{12,4},{1,9},{5,13},{9,1},{13,5},{2,10},{6,14},... | collective-permute-start | bytes 940040 | tf_op jit(solution)/shard_map/ppermute | solution.py:112
  41.4 0.5 collective-permute-start.7
  41.9 0.0 collective-permute-done.6.refs_5_
  41.9 1.5 %collective-permute-start.8 = (bf16[136,1152]{1,0:T(8,128)(2,1)S(1)}, bf16[136,1152]{1,0:T(8,128)(2,1)S(1)}, u32[]{:S(2)}, u32[]{:S(2)}) collective-permute-start(bf16[136,1152]{1,0:T(8,128)(2,1)S(1)} %collective-permute-done.6.refs_5_), channel_id=1, source_target_pairs={{0,8},{4,12},{8,0},{12,4},{1,9},{5,13},{9,1},{13,5},{2,10},{6,14},... | collective-permute-start | bytes 940040 | tf_op jit(solution)/shard_map/ppermute | solution.py:112
  43.5 1.5 %collective-permute-start.14 = (bf16[136,1152]{1,0:T(8,128)(2,1)S(1)}, bf16[136,1152]{1,0:T(8,128)(2,1)S(1)}, u32[]{:S(2)}, u32[]{:S(2)}) collective-permute-start(bf16[136,1152]{1,0:T(8,128)(2,1)S(1)} %collective-permute-done.13.refs_12_), channel_id=1, source_target_pairs={{0,16},{16,0},{1,17},{17,1},{2,18},{18,2},{3,19},{19,3},{4,20},{20... | collective-permute-start | bytes 940040 | tf_op jit(solution)/shard_map/ppermute | solution.py:112
  44.9 0.2 collective-permute-start.3
  45.2 5.0 %collective-permute-done.15.refs_14_ = bf16[136,1152]{1,0:T(8,128)(2,1)S(1)} collective-permute-done((bf16[136,1152]{1,0:T(8,128)(2,1)S(1)}, bf16[136,1152]{1,0:T(8,128)(2,1)S(1)}, u32[]{:S(2)}, u32[]{:S(2)}) %collective-permute-start.15) | collective-permute-done | bytes 313376 | tf_op jit(solution)/shard_map/ppermute | solution.py:112
  50.2 1.5 %collective-permute-start.16 = (bf16[136,1152]{1,0:T(8,128)(2,1)S(1)}, bf16[136,1152]{1,0:T(8,128)(2,1)S(1)}, u32[]{:S(2)}, u32[]{:S(2)}) collective-permute-start(bf16[136,1152]{1,0:T(8,128)(2,1)S(1)} %collective-permute-done.15.refs_14_), channel_id=1, source_target_pairs={{0,16},{16,0},{1,17},{17,1},{2,18},{18,2},{3,19},{19,3},{4,20},{20... | collective-permute-start | bytes 940040 | tf_op jit(solution)/shard_map/ppermute | solution.py:112
  51.7 5.2 %collective-permute-done.7.refs_6_ = bf16[136,1152]{1,0:T(8,128)(2,1)S(1)} collective-permute-done((bf16[136,1152]{1,0:T(8,128)(2,1)S(1)}, bf16[136,1152]{1,0:T(8,128)(2,1)S(1)}, u32[]{:S(2)}, u32[]{:S(2)}) %collective-permute-start.7) | collective-permute-done | bytes 313376 | tf_op jit(solution)/shard_map/ppermute | solution.py:112
  56.9 0.0 collective-permute-start.9
  56.9 4.7 %collective-permute-done.8.refs_7_ = bf16[136,1152]{1,0:T(8,128)(2,1)S(1)} collective-permute-done((bf16[136,1152]{1,0:T(8,128)(2,1)S(1)}, bf16[136,1152]{1,0:T(8,128)(2,1)S(1)}, u32[]{:S(2)}, u32[]{:S(2)}) %collective-permute-start.8) | collective-permute-done | bytes 313376 | tf_op jit(solution)/shard_map/ppermute | solution.py:112
  61.7 0.0 collective-permute-start.10
  61.7 0.0 collective-permute-done.14.refs_13_
  61.7 0.5 collective-permute-start.11
  62.2 0.0 collective-permute-done.3.refs_0_.refs_1_
  62.2 0.0 collective-permute-start.4
  62.2 0.0 collective-permute-done.16.refs_15_
  62.2 0.2 collective-permute-start.12
  62.3 4.3 %collective-permute-done.4.refs_2_ = bf16[1076]{0:T(1024)(128)(2,1)S(1)} collective-permute-done((bf16[1076]{0:T(1024)(128)(2,1)S(1)}, bf16[1076]{0:T(1024)(128)(2,1)S(1)}, u32[]{:S(2)}, u32[]{:S(2)}) %collective-permute-start.4) | collective-permute-done | bytes 2184 | tf_op jit(solution)/shard_map/ppermute | solution.py:112
  66.7 0.0 collective-permute-start.17
  66.7 0.0 collective-permute-done.9.refs_8_
  66.7 0.5 collective-permute-start.18
  67.2 0.0 collective-permute-done.10.refs_9_
  67.2 0.1 collective-permute-start.19
  67.3 0.0 collective-permute-done.11.refs_10_
  67.3 0.4 collective-permute-start.20
  67.7 2.2 %shard_map.168.refs_3_ = f32[192,1152]{1,0:T(8,128)S(1)} custom-call(bf16[192,1152]{1,0:T(8,128)(2,1)S(1)} %collective-permute-done.3.refs_0_.refs_1_, bf16[1076,1152]{1,0:T(8,128)(2,1)S(1)} %bitcast.10, bf16[1076]{0:T(1024)(128)(2,1)S(1)} %copy-done.9, bf16[1076,1152]{1,0:T(8,128)(2,1)S(1)} %copy-done.3), custom_call_target="tpu_custom_call" | custom-call | flops 951975936 | tf_op jit(solution)/shard_map/pallas_call | solution.py:286
  69.9 0.0 collective-permute-done.12.refs_11_
  70.0 0.0 collective-permute-done.17.refs_16_
  70.0 0.0 collective-permute-done.18.refs_17_
  70.0 0.0 collective-permute-done.19.refs_18_
  70.0 0.0 collective-permute-done.20.refs_19_
  70.0 2.6 %shard_map.169 = bf16[192,1152]{1,0:T(8,128)(2,1)S(1)} custom-call(s32[1]{0:T(128)} %bitcast.refs_0_, bf16[192,1152]{1,0:T(8,128)(2,1)S(1)} %collective-permute-done.3.refs_0_.refs_1_, bf16[1076]{0:T(1024)(128)(2,1)S(1)} %collective-permute-done.4.refs_2_, f32[192,1152]{1,0:T(8,128)S(1)} %shard_map.168.refs_3_, ...), custom_call_target="tpu_custom_call" | custom-call | flops 951975936 | tf_op jit(solution)/shard_map/pallas_call | solution.py:286
  72.6 0.0 copy-start.10
  72.7 0.1 collective-permute-start.21
  72.7 2.2 %shard_map.170.refs_3_ = f32[192,1152]{1,0:T(8,128)S(1)} custom-call(bf16[192,1152]{1,0:T(8,128)(2,1)S(1)} %get-tuple-element.43.refs_0_.refs_1_, bf16[1076,1152]{1,0:T(8,128)(2,1)S(1)} %bitcast.11, bf16[1076]{0:T(1024)(128)(2,1)S(1)} %copy-done.9, bf16[1076,1152]{1,0:T(8,128)(2,1)S(1)} %copy-done.3), custom_call_target="tpu_custom_call" | custom-call | flops 951975936 | tf_op jit(solution)/shard_map/pallas_call | solution.py:286
  75.0 2.5 %shard_map.171 = f32[192,1152]{1,0:T(8,128)S(1)} custom-call(s32[1]{0:T(128)} %bitcast.refs_0_, bf16[192,1152]{1,0:T(8,128)(2,1)S(1)} %get-tuple-element.43.refs_0_.refs_1_, bf16[1076]{0:T(1024)(128)(2,1)S(1)} %collective-permute-done.4.refs_2_, f32[192,1152]{1,0:T(8,128)S(1)} %shard_map.170.refs_3_, bf16[136,1152]{1,0:T(8,128)(2,1)S(1)} %collective-permute-done.5.refs_4_, ...), custom_call_target="tpu_custom_call" | custom-call | flops 951975936 | tf_op jit(solution)/shard_map/pallas_call | solution.py:286
  77.5 7.4 %collective-permute-done.21 = bf16[192,1152]{1,0:T(8,128)(2,1)S(1)} collective-permute-done((bf16[192,1152]{1,0:T(8,128)(2,1)S(1)}, bf16[192,1152]{1,0:T(8,128)(2,1)S(1)}, u32[]{:S(2)}, u32[]{:S(2)}) %collective-permute-start.21) | collective-permute-done | bytes 442400 | tf_op jit(solution)/shard_map/ppermute | solution.py:112
  84.9 0.9 %fusion = bf16[1,192,1152]{2,1,0:T(8,128)(2,1)} fusion(f32[192,1152]{1,0:T(8,128)S(1)} %shard_map.171, bf16[192,1152]{1,0:T(8,128)(2,1)S(1)} %collective-permute-done.21), kind=kLoop, calls=%fused_computation.1 | loop fusion | flops 663552 | bytes 1769472 | tf_op jit(solution)/shard_map/broadcast_in_dim | solution.py:451
  (16 shorter events, 0.0 us)
Async XLA Ops:
  0.7 18.3 %collective-permute-start.1 = (s32[3,192]{1,0:T(4,128)S(1)}, s32[3,192]{1,0:T(4,128)S(1)}, u32[]{:S(2)}, u32[]{:S(2)}) collective-permute-start(s32[3,192]{1,0:T(4,128)S(1)} %pad_add_fusion.refs_1_.refs_3_.refs_2_), channel_id=1, source_target_pairs={{0,16},{16,0},{1,17},{17,1},{2,18},{18,2},{3,19},{19,3},{4,20},{20... | collective-permute-start | bytes 6920 | tf_op jit(solution)/shard_map/ppermute | solution.py:112
  4.8 20.4 %collective-permute-start.5 = (bf16[136,1152]{1,0:T(8,128)(2,1)S(1)}, bf16[136,1152]{1,0:T(8,128)(2,1)S(1)}, u32[]{:S(2)}, u32[]{:S(2)}) collective-permute-start(bf16[136,1152]{1,0:T(8,128)(2,1)S(1)} %dynamic-slice_bitcast_fusion), channel_id=1, source_target_pairs={{0,2},{1,3},{2,0},{3,1},{4,6},{5,7},{6,4},{7,5},{8,10},{9,11},{10,... | collective-permute-start | bytes 940040 | tf_op jit(solution)/shard_map/ppermute | solution.py:112
  7.5 11.6 %collective-permute-start = (bf16[192,1152]{1,0:T(8,128)(2,1)}, bf16[192,1152]{1,0:T(8,128)(2,1)S(1)}, u32[]{:S(2)}, u32[]{:S(2)}) collective-permute-start(bf16[192,1152]{1,0:T(8,128)(2,1)} %bitcast.12), channel_id=1, source_target_pairs={{0,16},{16,0},{1,17},{17,1},{2,18},{18,2},{3,19},{19,3},{4,20},{20... | collective-permute-start | bytes 1327112 | tf_op jit(solution)/shard_map/ppermute | solution.py:112
  9.1 2.1 %copy-start = (bf16[1152,1728]{0,1:T(8,128)(2,1)S(1)}, bf16[1152,1728]{0,1:T(8,128)(2,1)}, u32[]{:S(2)}) copy-start(bf16[1152,1728]{0,1:T(8,128)(2,1)} %param.25) | copy-start | bytes 11943940
  11.2 7.8 %copy-start.1 = (bf16[1152,1728]{0,1:T(8,128)(2,1)S(1)}, bf16[1152,1728]{0,1:T(8,128)(2,1)}, u32[]{:S(2)}) copy-start(bf16[1152,1728]{0,1:T(8,128)(2,1)} %param.25) | copy-start | bytes 11943940
  11.2 7.8 %copy-start.5 = (bf16[64,1152]{1,0:T(8,128)(2,1)S(1)}, bf16[64,1152]{1,0:T(8,128)(2,1)}, u32[]{:S(2)}) copy-start(bf16[64,1152]{1,0:T(8,128)(2,1)} %refs_2_.5) | copy-start | bytes 442372
  11.2 7.8 %copy-start.6 = (bf16[64,1152]{1,0:T(8,128)(2,1)S(1)}, bf16[64,1152]{1,0:T(8,128)(2,1)}, u32[]{:S(2)}) copy-start(bf16[64,1152]{1,0:T(8,128)(2,1)} %refs_3_.6) | copy-start | bytes 442372
  11.2 7.8 %copy-start.7 = (f32[1152]{0:T(1024)S(1)}, f32[1152]{0:T(1024)}, u32[]{:S(2)}) copy-start(f32[1152]{0:T(1024)} %refs_4_.6) | copy-start | bytes 13828
  11.2 7.8 %copy-start.8 = (f32[1152]{0:T(1024)S(1)}, f32[1152]{0:T(1024)}, u32[]{:S(2)}) copy-start(f32[1152]{0:T(1024)} %refs_5_.4) | copy-start | bytes 13828
  19.0 2.0 %copy-start.4 = (bf16[576,1152]{1,0:T(8,128)(2,1)S(1)}, bf16[576,1152]{1,0:T(8,128)(2,1)}, u32[]{:S(2)}) copy-start(bf16[576,1152]{1,0:T(8,128)(2,1)} %refs_4_.8) | copy-start | bytes 3981316
  24.2 38.0 %copy-start.9 = (bf16[1076]{0:T(1024)(128)(2,1)S(1)}, bf16[1076]{0:T(1024)(128)(2,1)}, u32[]{:S(2)}) copy-start(bf16[1076]{0:T(1024)(128)(2,1)} %refs_2_.7) | copy-start | bytes 6460
  24.2 43.5 %copy-start.2 = (bf16[1152,1076]{0,1:T(8,128)(2,1)S(1)}, bf16[1152,1076]{0,1:T(8,128)(2,1)}, u32[]{:S(2)}) copy-start(bf16[1152,1076]{0,1:T(8,128)(2,1)} %param.30) | copy-start | bytes 7437316
  24.2 43.5 %copy-start.3 = (bf16[1076,1152]{1,0:T(8,128)(2,1)S(1)}, bf16[1076,1152]{1,0:T(8,128)(2,1)}, u32[]{:S(2)}) copy-start(bf16[1076,1152]{1,0:T(8,128)(2,1)} %refs_3_.9) | copy-start | bytes 7437316
  24.3 13.1 %collective-permute-start.2 = (bf16[192,1152]{1,0:T(8,128)(2,1)S(1)}, bf16[192,1152]{1,0:T(8,128)(2,1)S(1)}, u32[]{:S(2)}, u32[]{:S(2)}) collective-permute-start(bf16[192,1152]{1,0:T(8,128)(2,1)S(1)} %shard_map.165), channel_id=1, source_target_pairs={{0,16},{16,0},{1,17},{17,1},{2,18},{18,2},{3,19},{19,3},{4,20},{20... | collective-permute-start | bytes 1327112 | tf_op jit(solution)/shard_map/ppermute | solution.py:112
  24.9 15.1 %collective-permute-start.13 = (bf16[136,1152]{1,0:T(8,128)(2,1)S(1)}, bf16[136,1152]{1,0:T(8,128)(2,1)S(1)}, u32[]{:S(2)}, u32[]{:S(2)}) collective-permute-start(bf16[136,1152]{1,0:T(8,128)(2,1)S(1)} %dynamic-slice_select_fusion), channel_id=1, source_target_pairs={{0,2},{1,3},{2,0},{3,1},{4,6},{5,7},{6,4},{7,5},{8,10},{9,11},{10,... | collective-permute-start | bytes 940040 | tf_op jit(solution)/shard_map/ppermute | solution.py:112
  25.2 16.7 %collective-permute-start.6 = (bf16[136,1152]{1,0:T(8,128)(2,1)S(1)}, bf16[136,1152]{1,0:T(8,128)(2,1)S(1)}, u32[]{:S(2)}, u32[]{:S(2)}) collective-permute-start(bf16[136,1152]{1,0:T(8,128)(2,1)S(1)} %collective-permute-done.5.refs_4_), channel_id=1, source_target_pairs={{0,16},{16,0},{1,17},{17,1},{2,18},{18,2},{3,19},{19,3},{4,20},{20... | collective-permute-start | bytes 940040 | tf_op jit(solution)/shard_map/ppermute | solution.py:112
  39.9 10.3 %collective-permute-start.15 = (bf16[136,1152]{1,0:T(8,128)(2,1)S(1)}, bf16[136,1152]{1,0:T(8,128)(2,1)S(1)}, u32[]{:S(2)}, u32[]{:S(2)}) collective-permute-start(bf16[136,1152]{1,0:T(8,128)(2,1)S(1)} %collective-permute-done.13.refs_12_), channel_id=1, source_target_pairs={{0,8},{4,12},{8,0},{12,4},{1,9},{5,13},{9,1},{13,5},{2,10},{6,14},... | collective-permute-start | bytes 940040 | tf_op jit(solution)/shard_map/ppermute | solution.py:112
  41.4 15.5 %collective-permute-start.7 = (bf16[136,1152]{1,0:T(8,128)(2,1)S(1)}, bf16[136,1152]{1,0:T(8,128)(2,1)S(1)}, u32[]{:S(2)}, u32[]{:S(2)}) collective-permute-start(bf16[136,1152]{1,0:T(8,128)(2,1)S(1)} %collective-permute-done.5.refs_4_), channel_id=1, source_target_pairs={{0,8},{4,12},{8,0},{12,4},{1,9},{5,13},{9,1},{13,5},{2,10},{6,14},... | collective-permute-start | bytes 940040 | tf_op jit(solution)/shard_map/ppermute | solution.py:112
  41.9 19.7 %collective-permute-start.8 = (bf16[136,1152]{1,0:T(8,128)(2,1)S(1)}, bf16[136,1152]{1,0:T(8,128)(2,1)S(1)}, u32[]{:S(2)}, u32[]{:S(2)}) collective-permute-start(bf16[136,1152]{1,0:T(8,128)(2,1)S(1)} %collective-permute-done.6.refs_5_), channel_id=1, source_target_pairs={{0,8},{4,12},{8,0},{12,4},{1,9},{5,13},{9,1},{13,5},{2,10},{6,14},... | collective-permute-start | bytes 940040 | tf_op jit(solution)/shard_map/ppermute | solution.py:112
  43.5 18.2 %collective-permute-start.14 = (bf16[136,1152]{1,0:T(8,128)(2,1)S(1)}, bf16[136,1152]{1,0:T(8,128)(2,1)S(1)}, u32[]{:S(2)}, u32[]{:S(2)}) collective-permute-start(bf16[136,1152]{1,0:T(8,128)(2,1)S(1)} %collective-permute-done.13.refs_12_), channel_id=1, source_target_pairs={{0,16},{16,0},{1,17},{17,1},{2,18},{18,2},{3,19},{19,3},{4,20},{20... | collective-permute-start | bytes 940040 | tf_op jit(solution)/shard_map/ppermute | solution.py:112
  44.9 17.2 %collective-permute-start.3 = (bf16[192,1152]{1,0:T(8,128)(2,1)S(1)}, bf16[192,1152]{1,0:T(8,128)(2,1)S(1)}, u32[]{:S(2)}, u32[]{:S(2)}) collective-permute-start(bf16[192,1152]{1,0:T(8,128)(2,1)S(1)} %get-tuple-element.43.refs_0_.refs_1_), channel_id=1, source_target_pairs={{0,1},{1,0},{2,3},{3,2},{4,5},{5,4},{6,7},{7,6},{8,9},{9,8},{10,11... | collective-permute-start | bytes 1327112 | tf_op jit(solution)/shard_map/ppermute | solution.py:112
  50.2 12.0 %collective-permute-start.16 = (bf16[136,1152]{1,0:T(8,128)(2,1)S(1)}, bf16[136,1152]{1,0:T(8,128)(2,1)S(1)}, u32[]{:S(2)}, u32[]{:S(2)}) collective-permute-start(bf16[136,1152]{1,0:T(8,128)(2,1)S(1)} %collective-permute-done.15.refs_14_), channel_id=1, source_target_pairs={{0,16},{16,0},{1,17},{17,1},{2,18},{18,2},{3,19},{19,3},{4,20},{20... | collective-permute-start | bytes 940040 | tf_op jit(solution)/shard_map/ppermute | solution.py:112
  56.9 9.8 %collective-permute-start.9 = (bf16[136,1152]{1,0:T(8,128)(2,1)S(1)}, bf16[136,1152]{1,0:T(8,128)(2,1)S(1)}, u32[]{:S(2)}, u32[]{:S(2)}) collective-permute-start(bf16[136,1152]{1,0:T(8,128)(2,1)S(1)} %collective-permute-done.5.refs_4_), channel_id=1, source_target_pairs={{0,4},{4,0},{8,12},{12,8},{1,5},{5,1},{9,13},{13,9},{2,6},{6,2},{1... | collective-permute-start | bytes 940040 | tf_op jit(solution)/shard_map/ppermute | solution.py:112
  61.7 5.5 %collective-permute-start.10 = (bf16[136,1152]{1,0:T(8,128)(2,1)S(1)}, bf16[136,1152]{1,0:T(8,128)(2,1)S(1)}, u32[]{:S(2)}, u32[]{:S(2)}) collective-permute-start(bf16[136,1152]{1,0:T(8,128)(2,1)S(1)} %collective-permute-done.6.refs_5_), channel_id=1, source_target_pairs={{0,4},{4,0},{8,12},{12,8},{1,5},{5,1},{9,13},{13,9},{2,6},{6,2},{1... | collective-permute-start | bytes 940040 | tf_op jit(solution)/shard_map/ppermute | solution.py:112
  61.7 5.6 %collective-permute-start.11 = (bf16[136,1152]{1,0:T(8,128)(2,1)S(1)}, bf16[136,1152]{1,0:T(8,128)(2,1)S(1)}, u32[]{:S(2)}, u32[]{:S(2)}) collective-permute-start(bf16[136,1152]{1,0:T(8,128)(2,1)S(1)} %collective-permute-done.7.refs_6_), channel_id=1, source_target_pairs={{0,4},{4,0},{8,12},{12,8},{1,5},{5,1},{9,13},{13,9},{2,6},{6,2},{1... | collective-permute-start | bytes 940040 | tf_op jit(solution)/shard_map/ppermute | solution.py:112
  62.2 4.5 %collective-permute-start.4 = (bf16[1076]{0:T(1024)(128)(2,1)S(1)}, bf16[1076]{0:T(1024)(128)(2,1)S(1)}, u32[]{:S(2)}, u32[]{:S(2)}) collective-permute-start(bf16[1076]{0:T(1024)(128)(2,1)S(1)} %copy-done.9), channel_id=1, source_target_pairs={{0,2},{1,3},{2,0},{3,1},{4,6},{5,7},{6,4},{7,5},{8,10},{9,11},{10,... | collective-permute-start | bytes 6464 | tf_op jit(solution)/shard_map/ppermute | solution.py:112
  62.2 7.8 %collective-permute-start.12 = (bf16[136,1152]{1,0:T(8,128)(2,1)S(1)}, bf16[136,1152]{1,0:T(8,128)(2,1)S(1)}, u32[]{:S(2)}, u32[]{:S(2)}) collective-permute-start(bf16[136,1152]{1,0:T(8,128)(2,1)S(1)} %collective-permute-done.8.refs_7_), channel_id=1, source_target_pairs={{0,4},{4,0},{8,12},{12,8},{1,5},{5,1},{9,13},{13,9},{2,6},{6,2},{1... | collective-permute-start | bytes 940040 | tf_op jit(solution)/shard_map/ppermute | solution.py:112
  66.7 3.3 %collective-permute-start.17 = (bf16[136,1152]{1,0:T(8,128)(2,1)S(1)}, bf16[136,1152]{1,0:T(8,128)(2,1)S(1)}, u32[]{:S(2)}, u32[]{:S(2)}) collective-permute-start(bf16[136,1152]{1,0:T(8,128)(2,1)S(1)} %collective-permute-done.13.refs_12_), channel_id=1, source_target_pairs={{0,4},{4,0},{8,12},{12,8},{1,5},{5,1},{9,13},{13,9},{2,6},{6,2},{1... | collective-permute-start | bytes 940040 | tf_op jit(solution)/shard_map/ppermute | solution.py:112
  66.7 3.3 %collective-permute-start.18 = (bf16[136,1152]{1,0:T(8,128)(2,1)S(1)}, bf16[136,1152]{1,0:T(8,128)(2,1)S(1)}, u32[]{:S(2)}, u32[]{:S(2)}) collective-permute-start(bf16[136,1152]{1,0:T(8,128)(2,1)S(1)} %collective-permute-done.14.refs_13_), channel_id=1, source_target_pairs={{0,4},{4,0},{8,12},{12,8},{1,5},{5,1},{9,13},{13,9},{2,6},{6,2},{1... | collective-permute-start | bytes 940040 | tf_op jit(solution)/shard_map/ppermute | solution.py:112
  67.2 2.8 %collective-permute-start.19 = (bf16[136,1152]{1,0:T(8,128)(2,1)S(1)}, bf16[136,1152]{1,0:T(8,128)(2,1)S(1)}, u32[]{:S(2)}, u32[]{:S(2)}) collective-permute-start(bf16[136,1152]{1,0:T(8,128)(2,1)S(1)} %collective-permute-done.15.refs_14_), channel_id=1, source_target_pairs={{0,4},{4,0},{8,12},{12,8},{1,5},{5,1},{9,13},{13,9},{2,6},{6,2},{1... | collective-permute-start | bytes 940040 | tf_op jit(solution)/shard_map/ppermute | solution.py:112
  67.3 2.7 %collective-permute-start.20 = (bf16[136,1152]{1,0:T(8,128)(2,1)S(1)}, bf16[136,1152]{1,0:T(8,128)(2,1)S(1)}, u32[]{:S(2)}, u32[]{:S(2)}) collective-permute-start(bf16[136,1152]{1,0:T(8,128)(2,1)S(1)} %collective-permute-done.16.refs_15_), channel_id=1, source_target_pairs={{0,4},{4,0},{8,12},{12,8},{1,5},{5,1},{9,13},{13,9},{2,6},{6,2},{1... | collective-permute-start | bytes 940040 | tf_op jit(solution)/shard_map/ppermute | solution.py:112
  72.6 2.3 %copy-start.10 = (bf16[1152]{0:T(1024)(128)(2,1)S(1)}, bf16[1152]{0:T(1024)(128)(2,1)}, u32[]{:S(2)}) copy-start(bf16[1152]{0:T(1024)(128)(2,1)} %refs_21_.1) | copy-start | bytes 6916
  72.7 12.2 %collective-permute-start.21 = (bf16[192,1152]{1,0:T(8,128)(2,1)S(1)}, bf16[192,1152]{1,0:T(8,128)(2,1)S(1)}, u32[]{:S(2)}, u32[]{:S(2)}) collective-permute-start(bf16[192,1152]{1,0:T(8,128)(2,1)S(1)} %shard_map.169), channel_id=1, source_target_pairs={{0,1},{1,0},{2,3},{3,2},{4,5},{5,4},{6,7},{7,6},{8,9},{9,8},{10,11... | collective-permute-start | bytes 1327112 | tf_op jit(solution)/shard_map/ppermute | solution.py:112

commit v3 on v2

--- a/solution.py
+++ b/solution.py
@@ -135,7 +135,9 @@
     return moved * lax.rsqrt(spread + 1e-06) * gain + shift
 
 
-def project_kernel(patch, places, row_tab, col_tab, gain, shift, weight, out, *embedded):
+def project_kernel(
+    patch, places, row_tab, col_tab, gain, shift, weight, out, *embedded, arrive=None
+):
     tokens = patch.shape[0]
     grid = row_tab.shape[0]
     level = lax.broadcasted_iota(jnp.int32, (grid, tokens), 0)
@@ -147,6 +149,8 @@
         ref[...] = values
     normed = norm_rows(values, gain[...][None], shift[...][None]).astype(jnp.bfloat16)
     head_dim = out.shape[1]
+    if arrive:
+        arrive()
     product = dot_t(weight[...], normed)
     for part in range(out.shape[0]):
         out[part] = product[part * head_dim : (part + 1) * head_dim].astype(jnp.bfloat16)
@@ -159,28 +163,28 @@
     return jnp.sum(jnp.where(across == along, row, 0.0), -1, keepdims=True)
 
 
-def attend_kernel(near, far, near_places, far_places, weight, out, mixed):
+def attend_kernel(near, far, near_places, far_places, weight, out, mixed, scores, probs):
     head_dim = near.shape[1]
     heads = near.shape[0] // 3
     scale = math.log2(math.e) / math.sqrt(head_dim)
     segs = [places[2:3, :].astype(jnp.float32) for places in (near_places, far_places)]
-    same = [column_of(seg) == segs[0] for seg in segs]
+    bias = [jnp.where(column_of(seg) == segs[0], 0.0, -1e30) for seg in segs]
+    tokens = near.shape[2]
     for head in range(heads):
         query = near[3 * head]
-        scores = []
-        for side, keep in zip((near, far), same):
+        for i, side in enumerate((near, far)):
             raw = tn_dot(side[3 * head + 1], query)
-            scores.append(jnp.where(keep, raw, -1e30))
-        top = jnp.maximum(
-            jnp.max(scores[0], 0, keepdims=True), jnp.max(scores[1], 0, keepdims=True)
-        )
-        total = 0.0
-        result = 0.0
-        for side, raw in zip((near, far), scores):
-            expo = jnp.exp2((raw - top) * scale)
-            total = total + jnp.sum(expo, 0, keepdims=True)
-            result = result + wide_dot(side[3 * head + 2], expo.astype(jnp.bfloat16))
-        mixed[head * head_dim : (head + 1) * head_dim, :] = result / total
+            scores[head, i * tokens : (i + 1) * tokens, :] = raw + bias[i]
+    shares = []
+    for head in range(heads):
+        raw = scores[head]
+        expo = jnp.exp2((raw - jnp.max(raw, 0, keepdims=True)) * scale)
+        shares.append(1.0 / jnp.sum(expo, 0, keepdims=True))
+        probs[head] = expo.astype(jnp.bfloat16)
+    for head in range(heads):
+        result = wide_dot(near[3 * head + 2], probs[head, :tokens, :])
+        result = result + wide_dot(far[3 * head + 2], probs[head, tokens:, :])
+        mixed[head * head_dim : (head + 1) * head_dim, :] = result * shares[head]
     out[...] = tn_dot(mixed[...].astype(jnp.bfloat16), weight[...]).astype(out.dtype)
 
 
@@ -210,9 +214,9 @@
             total[...] += piece
 
 
-def far_mlp_kernel(count, extra, place, inputs, bias, total, *refs):
-    ups, downs = refs[:count], refs[count : 2 * count + extra]
-    rest = refs[2 * count + extra :]
+def far_mlp_kernel(count, picks, place, inputs, bias, total, *refs):
+    ups, downs = refs[: len(picks)], refs[len(picks) : 2 * len(picks)]
+    rest = refs[2 * len(picks) :]
     rows = ups[0].shape[0]
     hidden = bias.shape[0]
     line = bias[...].astype(jnp.float32)[None]
@@ -227,30 +231,28 @@
         bit *= 2
     order = [step ^ core for core in (0, 1) for step in spread_order(count)]
     up, down = rest[-2:]
-    for pieces, whole in ((ups, up), (downs, down)):
-        begin = 0
-        for piece in pieces:
-            whole[begin : begin + piece.shape[0], :] = piece[...]
-            begin += piece.shape[0]
+    for i in range(len(picks)):
+        up[i * rows : (i + 1) * rows, :] = ups[i][...]
+        down[i * rows : (i + 1) * rows, :] = downs[i][...]
     result = total[...]
-    group = count // 2
-    for half in range(2):
-        begin, end = half * group * rows, (half + 1) * group * rows
-        shift = jnp.concatenate([parts[j] for j in order[half * group : (half + 1) * group]], 1)
+    group = len(picks) // 2 if len(picks) == count else len(picks)
+    for first in range(0, len(picks), group):
+        begin, end = first * rows, (first + group) * rows
+        shift = jnp.concatenate([parts[order[p]] for p in picks[first : first + group]], 1)
         inner = dot_t(inputs[...], up[begin:end, :]) + shift
         result = result + wide_dot(gelu(inner).astype(jnp.bfloat16), down[begin:end, :])
     if len(rest) > 3:
         attended, last_bias, out = rest[:3]
         out[...] = result + attended[...] + last_bias[...].astype(jnp.float32)[None]
     else:
-        rest[0][...] = result.astype(jnp.bfloat16)
+        rest[0][...] = result.astype(rest[0].dtype)
 
 
 def spread_order(holders):
     return [0, holders // 2, 2, holders // 2 + 2]
 
 
-def run(kernel, room, out_shape, scratch=(), fetched=(), flops=0, scalars=()):
+def run(kernel, room, out_shape, scratch=(), fetched=(), late=(), flops=0, scalars=()):
     def call(*args):
         args = list(args)
         specs = []
@@ -278,8 +280,18 @@
                     refs[i] = extra[slot]
                 for copy in copies:
                     copy.start()
-                for copy in copies:
-                    copy.wait()
+                for slot, i in enumerate(fetched):
+                    if i not in late:
+                        copies[slot].wait()
+
+                def arrive():
+                    for slot, i in enumerate(fetched):
+                        if i in late:
+                            copies[slot].wait()
+
+                if late:
+                    kernel(*refs, arrive=arrive)
+                    return
             kernel(*refs)
 
         more = buffers + [pltpu.SemaphoreType.DMA((len(buffers),))] if fetched else []
@@ -384,14 +396,15 @@
             qkv_shape = pltpu.VMEM((3 * heads_here, head_dim, tokens), bf16)
             return run(
                 project_kernel,
-                8,
+                14,
                 (qkv_shape,) + more,
                 fetched=fetched,
+                late=(6,) if fetched else (),
                 flops=each * (qkv_rows.shape[0] + 256),
             )(values, where, row_table, col_table, ln1_gain, ln1_bias, qkv_rows)
 
         qkv_own, embedded = project(
-            after(patches[0], share1), places, (0, 2, 3, 4, 5), pltpu.VMEM(block, f32)
+            after(patches[0], share1), places, (0, 2, 3, 4, 5, 6), pltpu.VMEM(block, f32)
         )
         share2 = lax.dynamic_slice(after(w_fc2, share1), (begin, 0), (rows, width))
         repeated = (place == holders - 1) & (jnp.arange(rows) < overlap)
@@ -407,14 +420,18 @@
             return shares + [swap(share, "dp", dp, 1) for share in shares]
 
         def attend(near, far, near_places, far_places, shape):
-            scratch = [pltpu.VMEM((heads_here * head_dim, tokens), f32)]
-            return run(attend_kernel, 8, shape, scratch, flops=each * 2304)(
+            scratch = [
+                pltpu.VMEM((heads_here * head_dim, tokens), f32),
+                pltpu.VMEM((heads_here, 2 * tokens, tokens), f32),
+                pltpu.VMEM((heads_here, 2 * tokens, tokens), bf16),
+            ]
+            return run(attend_kernel, 14, shape, scratch, flops=each * 2304)(
                 near, far, near_places, far_places, w_out
             )
 
         sent = attend(qkv_other, qkv_own, places_other, places, sent_block)
+        far2 = swap(after(share2, sent), "tp", tp, 2)
         got = swap(sent, "seq", seq, 1)
-        far2 = swap(after(share2, sent), "tp", tp, 2)
         near1 = spread(after(far1, sent))
         kept = attend(after(qkv_own, sent), qkv_other, places, places_other, pltpu.VMEM(block, f32))
         attended, normed2 = run(
@@ -435,19 +452,30 @@
         theirs = mlp(partner)
         downs = cross([after(share, partner) for share in near2])
 
-        def far_mlp(values, total, shape, *tail):
+        def far_mlp(picks, values, total, shape, *tail):
+            pieces = [ups[p] for p in picks] + [downs[p] for p in picks]
             return run(
-                functools.partial(far_mlp_kernel, holders, len(downs) - holders),
+                functools.partial(far_mlp_kernel, holders, picks),
                 14,
                 shape,
-                [pltpu.VMEM((holders * rows, width), bf16)] * 2,
-                flops=2 * each * hidden,
+                [pltpu.VMEM((len(picks) * rows, width), bf16)] * 2,
+                flops=2 * each * len(picks) * rows,
                 scalars=(0,),
-            )(place[None], values, far_bias, total, *ups, *downs, *tail)
-
-        back = far_mlp(partner, theirs, sent_block)
+            )(place[None], values, far_bias, total, *pieces, *tail)
+
+        late = (holders // 2 - 1, holders - 1)
+        soon = tuple(p for p in range(holders) if p not in late)
+        theirs = far_mlp(soon, partner, theirs, pltpu.VMEM(block, f32))
+        back = far_mlp(late, partner, theirs, sent_block)
         returned = swap(back, "tp", tp, 1)
-        ours = far_mlp(after(normed2, back), mine, pltpu.VMEM(block, f32), attended, fc2_bias)
+        ours = far_mlp(
+            tuple(range(holders)),
+            after(normed2, back),
+            mine,
+            pltpu.VMEM(block, f32),
+            attended,
+            fc2_bias,
+        )
         return (ours + returned.astype(f32)).astype(bf16)[None]
 
     return per_device

time: 86 us -> 86.6 us (level)
  waiting for transfers between devices: 40.2 us -> 43.3 us
  local copies, waits for them, and re-layouts: 3.22 us -> 1.11 us
  Pallas kernels: 22.2 us -> 21.2 us
    ppermute x22, waiting for transfers between devices: 40.2 us -> 43.3 us  [swap(): return lax.ppermute(values, axis, [(i, i ^ bit) for i in range(size)])]
    unnamed x22 -> x20, local copies, waits for them, and re-layouts: 2.17 us -> 0.06 us
    pallas_call x9 -> x10, Pallas kernels: 22.2 us -> 21.2 us  [call(): pl.pallas_call(body, in_specs=specs, out_shape=out_shape, scratch_shapes=...]
  transfers between devices with their start and end apart: 22 -> 22, of which waited for: 8 -> 9; matrix products, arithmetic and copies ran while one was open for 3% -> 3% of each run, Pallas kernels for 23% -> 18%
where the time goes in v3:
time: 86.6 us; the launch traced here: 86.4 us
  waiting for transfers between devices  43.3 us (50%)
  Pallas kernels  21.2 us (24%)
  starting transfers between devices  17.9 us (21%)
  other arithmetic  2.7 us (3%)
  local copies, waits for them, and re-layouts  1.11 us (1%)
    ppermute x22, waiting for transfers between devices, swap(): return lax.ppermute(values, axis, [(i, i ^ bit) for i in range(size)])  43.3 us
    pallas_call x10, Pallas kernels, call(): pl.pallas_call(body, in_specs=specs, out_shape=out_shape, scratch_shapes=...  21.2 us
    ppermute x22, starting transfers between devices, swap(): return lax.ppermute(values, axis, [(i, i ^ bit) for i in range(size)])  17.9 us
  transfers between devices with their start and end apart: 22, of which 9 were waited for; matrix products, arithmetic and copies ran while one was open for 3% of the time, Pallas kernels for 18%

profile of v3, /device:TPU:0, one launch (start us, length us, event | category | flops | bytes accessed | tf_op | source)
XLA Modules:
  0.0 86.4 jit_solution(423460478536624071)
XLA Ops:
  0.0 0.7 pad_add_fusion.refs_1_.refs_3_.refs_2_
  0.7 3.0 %collective-permute-start.1 = (s32[3,192]{1,0:T(4,128)S(1)}, s32[3,192]{1,0:T(4,128)S(1)}, u32[]{:S(2)}, u32[]{:S(2)}) collective-permute-start(s32[3,192]{1,0:T(4,128)S(1)} %pad_add_fusion.refs_1_.refs_3_.refs_2_), channel_id=1, source_target_pairs={{0,16},{16,0},{1,17},{17,1},{2,18},{18,2},{3,19},{19,3},{4,20},{20... | collective-permute-start | bytes 6920 | tf_op jit(solution)/shard_map/ppermute | solution.py:112
  3.7 0.1 collective-permute-start
  3.8 1.1 %dynamic-slice_bitcast_fusion = bf16[136,1152]{1,0:T(8,128)(2,1)S(1)} fusion(bf16[1152,1076]{0,1:T(8,128)(2,1)} %param.30, s32[]{:T(128)S(6)} %select_n.8), kind=kLoop, calls=%fused_computation.3 | loop fusion | bytes 626692 | tf_op jit(solution)/shard_map/dynamic_slice | solution.py:391
  4.9 1.1 %dynamic-slice_select_fusion = bf16[136,1152]{1,0:T(8,128)(2,1)S(1)} fusion(bf16[1076,1152]{1,0:T(8,128)(2,1)} %refs_3_.9, s32[]{:T(128)S(6)} %select_n.8, pred[136]{0:T(512)(128)(4,1)S(1)} %compare_and_fusion), kind=kLoop, calls=%fused_computation.2 | loop fusion | flops 156672 | bytes 626828 | tf_op jit(solution)/shard_map/jit(_where)/select_n | solution.py:411
  6.0 0.0 copy-start
  6.0 0.0 copy-start.4
  6.0 0.0 copy-start.5
  6.0 0.0 copy-start.6
  6.0 0.0 copy-start.7
  6.1 3.9 %shard_map.163 = (bf16[24,72,192]{2,1,0:T(8,128)(2,1)S(1)}, f32[192,1152]{1,0:T(8,128)S(1)}) custom-call(bf16[192,1152]{1,0:T(8,128)(2,1)} %bitcast.13, s32[3,192]{1,0:T(4,128)S(1)} %pad_add_fusion.refs_1_.refs_3_.refs_2_, bf16[64,1152]{1,0:T(8,128)(2,1)} %refs_2_.5, bf16[64,1152]{1,0:T(8,128)(2,1)} %refs_3_.6, f32[1152]{0:T(1024)} %refs_4_.6, ...), custom_call_target="tpu_custom_call" | custom-call | flops 877658112 | tf_op jit(solution)/shard_map/pallas_call | solution.py:298
  10.0 5.6 %collective-permute-done.refs_0_ = bf16[192,1152]{1,0:T(8,128)(2,1)S(1)} collective-permute-done((bf16[192,1152]{1,0:T(8,128)(2,1)}, bf16[192,1152]{1,0:T(8,128)(2,1)S(1)}, u32[]{:S(2)}, u32[]{:S(2)}) %collective-permute-start) | collective-permute-done | bytes 442400 | tf_op jit(solution)/shard_map/ppermute | solution.py:112
  15.6 0.0 collective-permute-done.1.refs_1_.refs_2_.refs_3_
  15.6 1.9 %shard_map.164.refs_0_.refs_1_ = bf16[24,72,192]{2,1,0:T(8,128)(2,1)S(1)} custom-call(bf16[192,1152]{1,0:T(8,128)(2,1)S(1)} %collective-permute-done.refs_0_, s32[3,192]{1,0:T(4,128)S(1)} %collective-permute-done.1.refs_1_.refs_2_.refs_3_, bf16[64,1152]{1,0:T(8,128)(2,1)S(1)} %copy-done.4, bf16[64,1152]{1,0:T(8,128)(2,1)S(1)} %copy-done.5, ...), custom_call_target="tpu_custom_call" | custom-call | flops 877658112 | tf_op jit(solution)/shard_map/pallas_call | solution.py:298
  17.6 2.3 %shard_map.165 = bf16[192,1152]{1,0:T(8,128)(2,1)S(1)} custom-call(bf16[24,72,192]{2,1,0:T(8,128)(2,1)S(1)} %shard_map.164.refs_0_.refs_1_, bf16[24,72,192]{2,1,0:T(8,128)(2,1)S(1)} %get-tuple-element.30.refs_1_.refs_0_, s32[3,192]{1,0:T(4,128)S(1)} %collective-permute-done.1.refs_1_.refs_2_.refs_3_, s32[3,192]{1,0:T(4,128)S(1)} %pad_add_fusion.refs_1_.refs_3_.refs_2_, ...), custom_call_target="tpu_custom_call" | custom-call | flops 1019215872 | tf_op jit(solution)/shard_map/pallas_call | solution.py:298
  19.9 0.0 copy-start.8
  19.9 0.0 copy-start.1
  19.9 0.0 copy-start.2
  19.9 0.5 collective-permute-start.2
  20.4 2.8 %collective-permute-start.5 = (bf16[136,1152]{1,0:T(8,128)(2,1)S(1)}, bf16[136,1152]{1,0:T(8,128)(2,1)S(1)}, u32[]{:S(2)}, u32[]{:S(2)}) collective-permute-start(bf16[136,1152]{1,0:T(8,128)(2,1)S(1)} %dynamic-slice_bitcast_fusion), channel_id=1, source_target_pairs={{0,2},{1,3},{2,0},{3,1},{4,6},{5,7},{6,4},{7,5},{8,10},{9,11},{10,... | collective-permute-start | bytes 940040 | tf_op jit(solution)/shard_map/ppermute | solution.py:112
  23.2 0.1 collective-permute-start.11
  23.3 2.3 %shard_map.166.refs_1_ = f32[192,1152]{1,0:T(8,128)S(1)} custom-call(bf16[24,72,192]{2,1,0:T(8,128)(2,1)S(1)} %get-tuple-element.30.refs_1_.refs_0_, bf16[24,72,192]{2,1,0:T(8,128)(2,1)S(1)} %shard_map.164.refs_0_.refs_1_, s32[3,192]{1,0:T(4,128)S(1)} %pad_add_fusion.refs_1_.refs_3_.refs_2_, s32[3,192]{1,0:T(4,128)S(1)} %collective-permute-done.1.refs_1_.refs_2_.refs_3_, ...), custom_call_target="tpu_custom_call" | custom-call | flops 1019215872 | tf_op jit(solution)/shard_map/pallas_call | solution.py:298
  25.6 5.1 %collective-permute-done.2.refs_2_ = bf16[192,1152]{1,0:T(8,128)(2,1)S(1)} collective-permute-done((bf16[192,1152]{1,0:T(8,128)(2,1)S(1)}, bf16[192,1152]{1,0:T(8,128)(2,1)S(1)}, u32[]{:S(2)}, u32[]{:S(2)}) %collective-permute-start.2) | collective-permute-done | bytes 442400 | tf_op jit(solution)/shard_map/ppermute | solution.py:112
  30.8 1.1 %shard_map.167 = (f32[192,1152]{1,0:T(8,128)S(1)}, bf16[192,1152]{1,0:T(8,128)(2,1)S(1)}) custom-call(f32[192,1152]{1,0:T(8,128)S(1)} %get-tuple-element.26.refs_0_, f32[192,1152]{1,0:T(8,128)S(1)} %shard_map.166.refs_1_, bf16[192,1152]{1,0:T(8,128)(2,1)S(1)} %collective-permute-done.2.refs_2_, bf16[1152]{0:T(1024)(128)(2,1)} %refs_3_.7, f32[1152]{0:T(1024)} %refs_4_.9, ...), custom_call_target="tpu_custom_call" | custom-call | flops 28311552 | tf_op jit(solution)/shard_map/pallas_call | solution.py:298
  31.9 1.6 %collective-permute-start.3 = (bf16[192,1152]{1,0:T(8,128)(2,1)S(1)}, bf16[192,1152]{1,0:T(8,128)(2,1)S(1)}, u32[]{:S(2)}, u32[]{:S(2)}) collective-permute-start(bf16[192,1152]{1,0:T(8,128)(2,1)S(1)} %get-tuple-element.43.refs_0_.refs_1_), channel_id=1, source_target_pairs={{0,1},{1,0},{2,3},{3,2},{4,5},{5,4},{6,7},{7,6},{8,9},{9,8},{10,11... | collective-permute-start | bytes 1327112 | tf_op jit(solution)/shard_map/ppermute | solution.py:112
  33.5 10.3 %collective-permute-done.5.refs_4_ = bf16[136,1152]{1,0:T(8,128)(2,1)S(1)} collective-permute-done((bf16[136,1152]{1,0:T(8,128)(2,1)S(1)}, bf16[136,1152]{1,0:T(8,128)(2,1)S(1)}, u32[]{:S(2)}, u32[]{:S(2)}) %collective-permute-start.5) | collective-permute-done | bytes 313376 | tf_op jit(solution)/shard_map/ppermute | solution.py:112
  43.9 1.4 %collective-permute-start.6 = (bf16[136,1152]{1,0:T(8,128)(2,1)S(1)}, bf16[136,1152]{1,0:T(8,128)(2,1)S(1)}, u32[]{:S(2)}, u32[]{:S(2)}) collective-permute-start(bf16[136,1152]{1,0:T(8,128)(2,1)S(1)} %collective-permute-done.5.refs_4_), channel_id=1, source_target_pairs={{0,16},{16,0},{1,17},{17,1},{2,18},{18,2},{3,19},{19,3},{4,20},{20... | collective-permute-start | bytes 940040 | tf_op jit(solution)/shard_map/ppermute | solution.py:112
  45.3 1.5 %collective-permute-start.7 = (bf16[136,1152]{1,0:T(8,128)(2,1)S(1)}, bf16[136,1152]{1,0:T(8,128)(2,1)S(1)}, u32[]{:S(2)}, u32[]{:S(2)}) collective-permute-start(bf16[136,1152]{1,0:T(8,128)(2,1)S(1)} %collective-permute-done.5.refs_4_), channel_id=1, source_target_pairs={{0,8},{4,12},{8,0},{12,4},{1,9},{5,13},{9,1},{13,5},{2,10},{6,14},... | collective-permute-start | bytes 940040 | tf_op jit(solution)/shard_map/ppermute | solution.py:112
  46.8 2.8 %collective-permute-done.11.refs_10_.refs_12_ = bf16[136,1152]{1,0:T(8,128)(2,1)S(1)} collective-permute-done((bf16[136,1152]{1,0:T(8,128)(2,1)S(1)}, bf16[136,1152]{1,0:T(8,128)(2,1)S(1)}, u32[]{:S(2)}, u32[]{:S(2)}) %collective-permute-start.11) | collective-permute-done | bytes 313376 | tf_op jit(solution)/shard_map/ppermute | solution.py:112
  49.6 1.4 %collective-permute-start.13 = (bf16[136,1152]{1,0:T(8,128)(2,1)S(1)}, bf16[136,1152]{1,0:T(8,128)(2,1)S(1)}, u32[]{:S(2)}, u32[]{:S(2)}) collective-permute-start(bf16[136,1152]{1,0:T(8,128)(2,1)S(1)} %collective-permute-done.11.refs_10_.refs_12_), channel_id=1, source_target_pairs={{0,8},{4,12},{8,0},{12,4},{1,9},{5,13},{9,1},{13,5},{2,10},{6,14},... | collective-permute-start | bytes 940040 | tf_op jit(solution)/shard_map/ppermute | solution.py:112
  51.0 1.4 %collective-permute-start.12 = (bf16[136,1152]{1,0:T(8,128)(2,1)S(1)}, bf16[136,1152]{1,0:T(8,128)(2,1)S(1)}, u32[]{:S(2)}, u32[]{:S(2)}) collective-permute-start(bf16[136,1152]{1,0:T(8,128)(2,1)S(1)} %collective-permute-done.11.refs_10_.refs_12_), channel_id=1, source_target_pairs={{0,16},{16,0},{1,17},{17,1},{2,18},{18,2},{3,19},{19,3},{4,20},{20... | collective-permute-start | bytes 940040 | tf_op jit(solution)/shard_map/ppermute | solution.py:112
  52.4 0.0 collective-permute-done.6.refs_5_
  52.4 0.0 collective-permute-start.4
  52.4 4.5 %collective-permute-done.4.refs_2_ = bf16[1076]{0:T(1024)(128)(2,1)S(1)} collective-permute-done((bf16[1076]{0:T(1024)(128)(2,1)S(1)}, bf16[1076]{0:T(1024)(128)(2,1)S(1)}, u32[]{:S(2)}, u32[]{:S(2)}) %collective-permute-start.4) | collective-permute-done | bytes 2184 | tf_op jit(solution)/shard_map/ppermute | solution.py:112
  56.9 0.0 collective-permute-start.8
  56.9 0.0 collective-permute-done.7.refs_6_
  56.9 0.5 collective-permute-start.17
  57.4 1.5 %collective-permute-done.13.refs_12_.refs_14_ = bf16[136,1152]{1,0:T(8,128)(2,1)S(1)} collective-permute-done((bf16[136,1152]{1,0:T(8,128)(2,1)S(1)}, bf16[136,1152]{1,0:T(8,128)(2,1)S(1)}, u32[]{:S(2)}, u32[]{:S(2)}) %collective-permute-start.13) | collective-permute-done | bytes 313376 | tf_op jit(solution)/shard_map/ppermute | solution.py:112
  58.9 0.8 collective-permute-start.19
  59.7 0.0 collective-permute-done.12.refs_11_.refs_13_
  59.7 0.0 collective-permute-start.9
  59.7 0.0 collective-permute-done.3.refs_0_.refs_1_
  59.7 0.5 collective-permute-start.10
  60.2 0.0 collective-permute-done.8.refs_7_.refs_8_
  60.2 0.1 collective-permute-start.14
  60.3 6.4 %collective-permute-done.17.refs_4_.refs_7_ = bf16[136,1152]{1,0:T(8,128)(2,1)S(1)} collective-permute-done((bf16[136,1152]{1,0:T(8,128)(2,1)S(1)}, bf16[136,1152]{1,0:T(8,128)(2,1)S(1)}, u32[]{:S(2)}, u32[]{:S(2)}) %collective-permute-start.17) | collective-permute-done | bytes 313376 | tf_op jit(solution)/shard_map/ppermute | solution.py:112
  66.7 0.0 collective-permute-start.15
  66.7 0.6 collective-permute-done.19.refs_6_.refs_15_
  67.4 0.0 collective-permute-start.16
  67.4 0.0 collective-permute-done.9.refs_8_.refs_9_
  67.4 0.5 collective-permute-start.18
  67.9 0.1 collective-permute-start.20
  68.0 2.2 %shard_map.168.refs_3_ = f32[192,1152]{1,0:T(8,128)S(1)} custom-call(bf16[192,1152]{1,0:T(8,128)(2,1)S(1)} %collective-permute-done.3.refs_0_.refs_1_, bf16[1076,1152]{1,0:T(8,128)(2,1)S(1)} %bitcast.10, bf16[1076]{0:T(1024)(128)(2,1)S(1)} %copy-done.8, bf16[1076,1152]{1,0:T(8,128)(2,1)S(1)} %copy-done.2), custom_call_target="tpu_custom_call" | custom-call | flops 951975936 | tf_op jit(solution)/shard_map/pallas_call | solution.py:298
  70.2 0.0 collective-permute-done.16.refs_15_.refs_18_
  70.2 1.6 %shard_map.169.refs_3_ = f32[192,1152]{1,0:T(8,128)S(1)} custom-call(s32[1]{0:T(128)} %bitcast.refs_0_, bf16[192,1152]{1,0:T(8,128)(2,1)S(1)} %collective-permute-done.3.refs_0_.refs_1_, bf16[1076]{0:T(1024)(128)(2,1)S(1)} %collective-permute-done.4.refs_2_, f32[192,1152]{1,0:T(8,128)S(1)} %shard_map.168.refs_3_, ...), custom_call_target="tpu_custom_call" | custom-call | flops 721944576 | tf_op jit(solution)/shard_map/pallas_call | solution.py:298
  71.8 0.0 collective-permute-done.18.refs_5_.refs_11_
  71.8 0.0 collective-permute-done.20.refs_7_.refs_19_
  71.8 1.1 %shard_map.170 = bf16[192,1152]{1,0:T(8,128)(2,1)S(1)} custom-call(s32[1]{0:T(128)} %bitcast.refs_0_, bf16[192,1152]{1,0:T(8,128)(2,1)S(1)} %collective-permute-done.3.refs_0_.refs_1_, bf16[1076]{0:T(1024)(128)(2,1)S(1)} %collective-permute-done.4.refs_2_, f32[192,1152]{1,0:T(8,128)S(1)} %shard_map.169.refs_3_, ...), custom_call_target="tpu_custom_call" | custom-call | flops 240648192 | tf_op jit(solution)/shard_map/pallas_call | solution.py:298
  73.0 0.0 copy-start.9
  73.0 1.5 %collective-permute-start.21 = (bf16[192,1152]{1,0:T(8,128)(2,1)S(1)}, bf16[192,1152]{1,0:T(8,128)(2,1)S(1)}, u32[]{:S(2)}, u32[]{:S(2)}) collective-permute-start(bf16[192,1152]{1,0:T(8,128)(2,1)S(1)} %shard_map.170), channel_id=1, source_target_pairs={{0,1},{1,0},{2,3},{3,2},{4,5},{5,4},{6,7},{7,6},{8,9},{9,8},{10,11... | collective-permute-start | bytes 1327112 | tf_op jit(solution)/shard_map/ppermute | solution.py:112
  74.5 2.2 %shard_map.171.refs_3_ = f32[192,1152]{1,0:T(8,128)S(1)} custom-call(bf16[192,1152]{1,0:T(8,128)(2,1)S(1)} %get-tuple-element.43.refs_0_.refs_1_, bf16[1076,1152]{1,0:T(8,128)(2,1)S(1)} %bitcast.11, bf16[1076]{0:T(1024)(128)(2,1)S(1)} %copy-done.8, bf16[1076,1152]{1,0:T(8,128)(2,1)S(1)} %copy-done.2), custom_call_target="tpu_custom_call" | custom-call | flops 951975936 | tf_op jit(solution)/shard_map/pallas_call | solution.py:298
  76.7 2.5 %shard_map.172 = f32[192,1152]{1,0:T(8,128)S(1)} custom-call(s32[1]{0:T(128)} %bitcast.refs_0_, bf16[192,1152]{1,0:T(8,128)(2,1)S(1)} %get-tuple-element.43.refs_0_.refs_1_, bf16[1076]{0:T(1024)(128)(2,1)S(1)} %collective-permute-done.4.refs_2_, f32[192,1152]{1,0:T(8,128)S(1)} %shard_map.171.refs_3_, bf16[136,1152]{1,0:T(8,128)(2,1)S(1)} %collective-permute-done.5.refs_4_, ...), custom_call_target="tpu_custom_call" | custom-call | flops 962592768 | tf_op jit(solution)/shard_map/pallas_call | solution.py:298
  79.2 6.3 %collective-permute-done.21 = bf16[192,1152]{1,0:T(8,128)(2,1)S(1)} collective-permute-done((bf16[192,1152]{1,0:T(8,128)(2,1)S(1)}, bf16[192,1152]{1,0:T(8,128)(2,1)S(1)}, u32[]{:S(2)}, u32[]{:S(2)}) %collective-permute-start.21) | collective-permute-done | bytes 442400 | tf_op jit(solution)/shard_map/ppermute | solution.py:112
  85.5 0.9 %fusion = bf16[1,192,1152]{2,1,0:T(8,128)(2,1)} fusion(f32[192,1152]{1,0:T(8,128)S(1)} %shard_map.172, bf16[192,1152]{1,0:T(8,128)(2,1)S(1)} %collective-permute-done.21), kind=kLoop, calls=%fused_computation.1 | loop fusion | flops 663552 | bytes 1769472 | tf_op jit(solution)/shard_map/broadcast_in_dim | solution.py:479
  (15 shorter events, 0.0 us)
Async XLA Ops:
  0.7 14.9 %collective-permute-start.1 = (s32[3,192]{1,0:T(4,128)S(1)}, s32[3,192]{1,0:T(4,128)S(1)}, u32[]{:S(2)}, u32[]{:S(2)}) collective-permute-start(s32[3,192]{1,0:T(4,128)S(1)} %pad_add_fusion.refs_1_.refs_3_.refs_2_), channel_id=1, source_target_pairs={{0,16},{16,0},{1,17},{17,1},{2,18},{18,2},{3,19},{19,3},{4,20},{20... | collective-permute-start | bytes 6920 | tf_op jit(solution)/shard_map/ppermute | solution.py:112
  3.7 11.8 %collective-permute-start = (bf16[192,1152]{1,0:T(8,128)(2,1)}, bf16[192,1152]{1,0:T(8,128)(2,1)S(1)}, u32[]{:S(2)}, u32[]{:S(2)}) collective-permute-start(bf16[192,1152]{1,0:T(8,128)(2,1)} %bitcast.12), channel_id=1, source_target_pairs={{0,16},{16,0},{1,17},{17,1},{2,18},{18,2},{3,19},{19,3},{4,20},{20... | collective-permute-start | bytes 1327112 | tf_op jit(solution)/shard_map/ppermute | solution.py:112
  6.0 9.6 %copy-start = (bf16[1152,1728]{0,1:T(8,128)(2,1)S(1)}, bf16[1152,1728]{0,1:T(8,128)(2,1)}, u32[]{:S(2)}) copy-start(bf16[1152,1728]{0,1:T(8,128)(2,1)} %param.25) | copy-start | bytes 11943940
  6.0 9.6 %copy-start.4 = (bf16[64,1152]{1,0:T(8,128)(2,1)S(1)}, bf16[64,1152]{1,0:T(8,128)(2,1)}, u32[]{:S(2)}) copy-start(bf16[64,1152]{1,0:T(8,128)(2,1)} %refs_2_.5) | copy-start | bytes 442372
  6.0 9.6 %copy-start.5 = (bf16[64,1152]{1,0:T(8,128)(2,1)S(1)}, bf16[64,1152]{1,0:T(8,128)(2,1)}, u32[]{:S(2)}) copy-start(bf16[64,1152]{1,0:T(8,128)(2,1)} %refs_3_.6) | copy-start | bytes 442372
  6.0 9.6 %copy-start.6 = (f32[1152]{0:T(1024)S(1)}, f32[1152]{0:T(1024)}, u32[]{:S(2)}) copy-start(f32[1152]{0:T(1024)} %refs_4_.6) | copy-start | bytes 13828
  6.0 9.6 %copy-start.7 = (f32[1152]{0:T(1024)S(1)}, f32[1152]{0:T(1024)}, u32[]{:S(2)}) copy-start(f32[1152]{0:T(1024)} %refs_5_.4) | copy-start | bytes 13828
  15.6 2.0 %copy-start.3 = (bf16[576,1152]{1,0:T(8,128)(2,1)S(1)}, bf16[576,1152]{1,0:T(8,128)(2,1)}, u32[]{:S(2)}) copy-start(bf16[576,1152]{1,0:T(8,128)(2,1)} %refs_4_.8) | copy-start | bytes 3981316
  19.9 32.5 %copy-start.8 = (bf16[1076]{0:T(1024)(128)(2,1)S(1)}, bf16[1076]{0:T(1024)(128)(2,1)}, u32[]{:S(2)}) copy-start(bf16[1076]{0:T(1024)(128)(2,1)} %refs_2_.7) | copy-start | bytes 6460
  19.9 48.1 %copy-start.1 = (bf16[1152,1076]{0,1:T(8,128)(2,1)S(1)}, bf16[1152,1076]{0,1:T(8,128)(2,1)}, u32[]{:S(2)}) copy-start(bf16[1152,1076]{0,1:T(8,128)(2,1)} %param.30) | copy-start | bytes 7437316
  19.9 48.1 %copy-start.2 = (bf16[1076,1152]{1,0:T(8,128)(2,1)S(1)}, bf16[1076,1152]{1,0:T(8,128)(2,1)}, u32[]{:S(2)}) copy-start(bf16[1076,1152]{1,0:T(8,128)(2,1)} %refs_3_.9) | copy-start | bytes 7437316
  19.9 10.8 %collective-permute-start.2 = (bf16[192,1152]{1,0:T(8,128)(2,1)S(1)}, bf16[192,1152]{1,0:T(8,128)(2,1)S(1)}, u32[]{:S(2)}, u32[]{:S(2)}) collective-permute-start(bf16[192,1152]{1,0:T(8,128)(2,1)S(1)} %shard_map.165), channel_id=1, source_target_pairs={{0,16},{16,0},{1,17},{17,1},{2,18},{18,2},{3,19},{19,3},{4,20},{20... | collective-permute-start | bytes 1327112 | tf_op jit(solution)/shard_map/ppermute | solution.py:112
  20.4 23.5 %collective-permute-start.5 = (bf16[136,1152]{1,0:T(8,128)(2,1)S(1)}, bf16[136,1152]{1,0:T(8,128)(2,1)S(1)}, u32[]{:S(2)}, u32[]{:S(2)}) collective-permute-start(bf16[136,1152]{1,0:T(8,128)(2,1)S(1)} %dynamic-slice_bitcast_fusion), channel_id=1, source_target_pairs={{0,2},{1,3},{2,0},{3,1},{4,6},{5,7},{6,4},{7,5},{8,10},{9,11},{10,... | collective-permute-start | bytes 940040 | tf_op jit(solution)/shard_map/ppermute | solution.py:112
  23.2 26.4 %collective-permute-start.11 = (bf16[136,1152]{1,0:T(8,128)(2,1)S(1)}, bf16[136,1152]{1,0:T(8,128)(2,1)S(1)}, u32[]{:S(2)}, u32[]{:S(2)}) collective-permute-start(bf16[136,1152]{1,0:T(8,128)(2,1)S(1)} %dynamic-slice_select_fusion), channel_id=1, source_target_pairs={{0,2},{1,3},{2,0},{3,1},{4,6},{5,7},{6,4},{7,5},{8,10},{9,11},{10,... | collective-permute-start | bytes 940040 | tf_op jit(solution)/shard_map/ppermute | solution.py:112
  31.9 27.8 %collective-permute-start.3 = (bf16[192,1152]{1,0:T(8,128)(2,1)S(1)}, bf16[192,1152]{1,0:T(8,128)(2,1)S(1)}, u32[]{:S(2)}, u32[]{:S(2)}) collective-permute-start(bf16[192,1152]{1,0:T(8,128)(2,1)S(1)} %get-tuple-element.43.refs_0_.refs_1_), channel_id=1, source_target_pairs={{0,1},{1,0},{2,3},{3,2},{4,5},{5,4},{6,7},{7,6},{8,9},{9,8},{10,11... | collective-permute-start | bytes 1327112 | tf_op jit(solution)/shard_map/ppermute | solution.py:112
  43.9 8.5 %collective-permute-start.6 = (bf16[136,1152]{1,0:T(8,128)(2,1)S(1)}, bf16[136,1152]{1,0:T(8,128)(2,1)S(1)}, u32[]{:S(2)}, u32[]{:S(2)}) collective-permute-start(bf16[136,1152]{1,0:T(8,128)(2,1)S(1)} %collective-permute-done.5.refs_4_), channel_id=1, source_target_pairs={{0,16},{16,0},{1,17},{17,1},{2,18},{18,2},{3,19},{19,3},{4,20},{20... | collective-permute-start | bytes 940040 | tf_op jit(solution)/shard_map/ppermute | solution.py:112
  45.3 11.6 %collective-permute-start.7 = (bf16[136,1152]{1,0:T(8,128)(2,1)S(1)}, bf16[136,1152]{1,0:T(8,128)(2,1)S(1)}, u32[]{:S(2)}, u32[]{:S(2)}) collective-permute-start(bf16[136,1152]{1,0:T(8,128)(2,1)S(1)} %collective-permute-done.5.refs_4_), channel_id=1, source_target_pairs={{0,8},{4,12},{8,0},{12,4},{1,9},{5,13},{9,1},{13,5},{2,10},{6,14},... | collective-permute-start | bytes 940040 | tf_op jit(solution)/shard_map/ppermute | solution.py:112
  49.6 9.3 %collective-permute-start.13 = (bf16[136,1152]{1,0:T(8,128)(2,1)S(1)}, bf16[136,1152]{1,0:T(8,128)(2,1)S(1)}, u32[]{:S(2)}, u32[]{:S(2)}) collective-permute-start(bf16[136,1152]{1,0:T(8,128)(2,1)S(1)} %collective-permute-done.11.refs_10_.refs_12_), channel_id=1, source_target_pairs={{0,8},{4,12},{8,0},{12,4},{1,9},{5,13},{9,1},{13,5},{2,10},{6,14},... | collective-permute-start | bytes 940040 | tf_op jit(solution)/shard_map/ppermute | solution.py:112
  51.0 8.7 %collective-permute-start.12 = (bf16[136,1152]{1,0:T(8,128)(2,1)S(1)}, bf16[136,1152]{1,0:T(8,128)(2,1)S(1)}, u32[]{:S(2)}, u32[]{:S(2)}) collective-permute-start(bf16[136,1152]{1,0:T(8,128)(2,1)S(1)} %collective-permute-done.11.refs_10_.refs_12_), channel_id=1, source_target_pairs={{0,16},{16,0},{1,17},{17,1},{2,18},{18,2},{3,19},{19,3},{4,20},{20... | collective-permute-start | bytes 940040 | tf_op jit(solution)/shard_map/ppermute | solution.py:112
  52.4 4.5 %collective-permute-start.4 = (bf16[1076]{0:T(1024)(128)(2,1)S(1)}, bf16[1076]{0:T(1024)(128)(2,1)S(1)}, u32[]{:S(2)}, u32[]{:S(2)}) collective-permute-start(bf16[1076]{0:T(1024)(128)(2,1)S(1)} %copy-done.8), channel_id=1, source_target_pairs={{0,2},{1,3},{2,0},{3,1},{4,6},{5,7},{6,4},{7,5},{8,10},{9,11},{10,... | collective-permute-start | bytes 6464 | tf_op jit(solution)/shard_map/ppermute | solution.py:112
  56.9 3.3 %collective-permute-start.8 = (bf16[136,1152]{1,0:T(8,128)(2,1)S(1)}, bf16[136,1152]{1,0:T(8,128)(2,1)S(1)}, u32[]{:S(2)}, u32[]{:S(2)}) collective-permute-start(bf16[136,1152]{1,0:T(8,128)(2,1)S(1)} %collective-permute-done.5.refs_4_), channel_id=1, source_target_pairs={{0,4},{4,0},{8,12},{12,8},{1,5},{5,1},{9,13},{13,9},{2,6},{6,2},{1... | collective-permute-start | bytes 940040 | tf_op jit(solution)/shard_map/ppermute | solution.py:112
  56.9 9.8 %collective-permute-start.17 = (bf16[136,1152]{1,0:T(8,128)(2,1)S(1)}, bf16[136,1152]{1,0:T(8,128)(2,1)S(1)}, u32[]{:S(2)}, u32[]{:S(2)}) collective-permute-start(bf16[136,1152]{1,0:T(8,128)(2,1)S(1)} %collective-permute-done.6.refs_5_), channel_id=1, source_target_pairs={{0,8},{4,12},{8,0},{12,4},{1,9},{5,13},{9,1},{13,5},{2,10},{6,14},... | collective-permute-start | bytes 940040 | tf_op jit(solution)/shard_map/ppermute | solution.py:112
  58.9 8.5 %collective-permute-start.19 = (bf16[136,1152]{1,0:T(8,128)(2,1)S(1)}, bf16[136,1152]{1,0:T(8,128)(2,1)S(1)}, u32[]{:S(2)}, u32[]{:S(2)}) collective-permute-start(bf16[136,1152]{1,0:T(8,128)(2,1)S(1)} %collective-permute-done.13.refs_12_.refs_14_), channel_id=1, source_target_pairs={{0,16},{16,0},{1,17},{17,1},{2,18},{18,2},{3,19},{19,3},{4,20},{20... | collective-permute-start | bytes 940040 | tf_op jit(solution)/shard_map/ppermute | solution.py:112
  59.7 7.7 %collective-permute-start.9 = (bf16[136,1152]{1,0:T(8,128)(2,1)S(1)}, bf16[136,1152]{1,0:T(8,128)(2,1)S(1)}, u32[]{:S(2)}, u32[]{:S(2)}) collective-permute-start(bf16[136,1152]{1,0:T(8,128)(2,1)S(1)} %collective-permute-done.6.refs_5_), channel_id=1, source_target_pairs={{0,4},{4,0},{8,12},{12,8},{1,5},{5,1},{9,13},{13,9},{2,6},{6,2},{1... | collective-permute-start | bytes 940040 | tf_op jit(solution)/shard_map/ppermute | solution.py:112
  59.7 8.2 %collective-permute-start.10 = (bf16[136,1152]{1,0:T(8,128)(2,1)S(1)}, bf16[136,1152]{1,0:T(8,128)(2,1)S(1)}, u32[]{:S(2)}, u32[]{:S(2)}) collective-permute-start(bf16[136,1152]{1,0:T(8,128)(2,1)S(1)} %collective-permute-done.7.refs_6_), channel_id=1, source_target_pairs={{0,4},{4,0},{8,12},{12,8},{1,5},{5,1},{9,13},{13,9},{2,6},{6,2},{1... | collective-permute-start | bytes 940040 | tf_op jit(solution)/shard_map/ppermute | solution.py:112
  60.2 10.0 %collective-permute-start.14 = (bf16[136,1152]{1,0:T(8,128)(2,1)S(1)}, bf16[136,1152]{1,0:T(8,128)(2,1)S(1)}, u32[]{:S(2)}, u32[]{:S(2)}) collective-permute-start(bf16[136,1152]{1,0:T(8,128)(2,1)S(1)} %collective-permute-done.11.refs_10_.refs_12_), channel_id=1, source_target_pairs={{0,4},{4,0},{8,12},{12,8},{1,5},{5,1},{9,13},{13,9},{2,6},{6,2},{1... | collective-permute-start | bytes 940040 | tf_op jit(solution)/shard_map/ppermute | solution.py:112
  66.7 3.5 %collective-permute-start.15 = (bf16[136,1152]{1,0:T(8,128)(2,1)S(1)}, bf16[136,1152]{1,0:T(8,128)(2,1)S(1)}, u32[]{:S(2)}, u32[]{:S(2)}) collective-permute-start(bf16[136,1152]{1,0:T(8,128)(2,1)S(1)} %collective-permute-done.12.refs_11_.refs_13_), channel_id=1, source_target_pairs={{0,4},{4,0},{8,12},{12,8},{1,5},{5,1},{9,13},{13,9},{2,6},{6,2},{1... | collective-permute-start | bytes 940040 | tf_op jit(solution)/shard_map/ppermute | solution.py:112
  67.4 2.8 %collective-permute-start.16 = (bf16[136,1152]{1,0:T(8,128)(2,1)S(1)}, bf16[136,1152]{1,0:T(8,128)(2,1)S(1)}, u32[]{:S(2)}, u32[]{:S(2)}) collective-permute-start(bf16[136,1152]{1,0:T(8,128)(2,1)S(1)} %collective-permute-done.13.refs_12_.refs_14_), channel_id=1, source_target_pairs={{0,4},{4,0},{8,12},{12,8},{1,5},{5,1},{9,13},{13,9},{2,6},{6,2},{1... | collective-permute-start | bytes 940040 | tf_op jit(solution)/shard_map/ppermute | solution.py:112
  67.4 4.4 %collective-permute-start.18 = (bf16[136,1152]{1,0:T(8,128)(2,1)S(1)}, bf16[136,1152]{1,0:T(8,128)(2,1)S(1)}, u32[]{:S(2)}, u32[]{:S(2)}) collective-permute-start(bf16[136,1152]{1,0:T(8,128)(2,1)S(1)} %collective-permute-done.17.refs_4_.refs_7_), channel_id=1, source_target_pairs={{0,4},{4,0},{8,12},{12,8},{1,5},{5,1},{9,13},{13,9},{2,6},{6,2},{1... | collective-permute-start | bytes 940040 | tf_op jit(solution)/shard_map/ppermute | solution.py:112
  67.9 3.9 %collective-permute-start.20 = (bf16[136,1152]{1,0:T(8,128)(2,1)S(1)}, bf16[136,1152]{1,0:T(8,128)(2,1)S(1)}, u32[]{:S(2)}, u32[]{:S(2)}) collective-permute-start(bf16[136,1152]{1,0:T(8,128)(2,1)S(1)} %collective-permute-done.19.refs_6_.refs_15_), channel_id=1, source_target_pairs={{0,4},{4,0},{8,12},{12,8},{1,5},{5,1},{9,13},{13,9},{2,6},{6,2},{1... | collective-permute-start | bytes 940040 | tf_op jit(solution)/shard_map/ppermute | solution.py:112
  73.0 3.8 %copy-start.9 = (bf16[1152]{0:T(1024)(128)(2,1)S(1)}, bf16[1152]{0:T(1024)(128)(2,1)}, u32[]{:S(2)}) copy-start(bf16[1152]{0:T(1024)(128)(2,1)} %refs_21_.1) | copy-start | bytes 6916
  73.0 12.6 %collective-permute-start.21 = (bf16[192,1152]{1,0:T(8,128)(2,1)S(1)}, bf16[192,1152]{1,0:T(8,128)(2,1)S(1)}, u32[]{:S(2)}, u32[]{:S(2)}) collective-permute-start(bf16[192,1152]{1,0:T(8,128)(2,1)S(1)} %shard_map.170), channel_id=1, source_target_pairs={{0,1},{1,0},{2,3},{3,2},{4,5},{5,4},{6,7},{7,6},{8,9},{9,8},{10,11... | collective-permute-start | bytes 1327112 | tf_op jit(solution)/shard_map/ppermute | solution.py:112
